TPU v7x, 32 devices: a whole 2x2x4 slice. The times are simulated.
32 devices in a mesh: parts: 2 (over x), shot: 2 (over core), space: 8 (over z, y).
Axes of the slice: x: 2, y: 2, z: 4, core: 2. Of those that a mesh axis runs over, the one named last changes fastest.
Arguments:
- image: float32 [3200, 2, 192], P(('parts', 'space')), parts along dimension 0, may hold values from -6 to 6
- coil_maps: bfloat16 [16, 3200, 2, 192], P(None, ('parts', 'space')), parts along dimension 1, may hold values from -1.5 to 1.5
- psf_phase: float32 [3200, 576], P(('parts', 'space')), parts along dimension 0, may hold values from -3.140625 to 3.140625
- line_mask: int32 [4, 200], P(('parts', 'shot')), parts along dimension 0, may hold values 0 or 1
- motion: int32 [4, 3], P(('parts', 'shot')), parts along dimension 0, may hold values from 0 to 16
Outputs:
- result: float32 [3200, 2, 192], P(('parts', 'space')), parts along dimension 0
There are 2 independent parts, one for each index of `parts`. A program takes and returns all parts, laid end to end along the dimension named above; each array names one. Nothing has to cross between parts.
Inputs may be any that keep to these rules, and one draw needn't show every extreme that they name: `motion`: column 0 selects the rotation angle, columns 1 and 2 the shifts along x and y.
All inputs are finite; a program needn't handle non-finite values. No bound on the sum of `line_mask` on one device may be relied on, other than what follows from the above.
Results may differ from a plain program's by a relative error of at most 0.003.
Values may be sent and summed in bfloat16 or wider, within the bound.
No kernel may reach another device: no remote copies, remote signals or barrier semaphores. Data moves between devices by JAX's collectives and lax.ppermute only.
A program may use at most 64 MiB of HBM per device.

v0:
```python
import functools

import jax
import jax.numpy as jnp
import numpy as np
from jax import lax
from jax.experimental import pallas as pl
from jax.experimental.pallas import tpu as pltpu
from jax.sharding import PartitionSpec as P

LEVELS = 17
ANGLE_STEP = 0.02
SHIFT_STEP = 0.5
LANES = 128
BF = jnp.bfloat16
F32 = jnp.float32


def split_pair(table):
    high = table.astype(np.float32).astype(BF)
    low = (table - high.astype(np.float64)).astype(np.float32).astype(BF)
    return np.stack([high, low])


def row_tables(width):
    index = np.arange(width)
    angle = 2 * np.pi * (np.outer(index, index) % width) / width
    return split_pair(np.concatenate([np.cos(angle), np.sin(angle)], 0) / np.sqrt(width))


def column_tables(length):
    half = length // 2
    result = []
    for parity in range(2):
        inputs = np.arange(half)[:, None]
        freqs = 2 * np.arange(half)[None, :] + parity
        angle = -2 * np.pi * (inputs * freqs % length) / length
        wave = np.exp(1j * angle) / np.sqrt(length)
        table = np.zeros((2 * LANES, 2 * LANES))
        table[:half, :half] = wave.real
        table[:half, LANES:LANES + half] = wave.imag
        table[LANES:LANES + half, :half] = -wave.imag
        table[LANES:LANES + half, LANES:LANES + half] = wave.real
        result.append(split_pair(table))
    return np.stack(result)


def readout_tables(width, readout):
    half = width // 2
    classes = readout // half
    pads, crops = [], []
    for j in range(classes):
        k = np.arange(half)[:, None] * classes + j
        x = np.arange(half)[None, :]
        angle = -2 * np.pi * (k * x % readout) / readout
        cosine = (np.cos(angle) / np.sqrt(readout)).astype(np.float32).astype(BF)
        sine = (np.sin(angle) / np.sqrt(readout)).astype(np.float32).astype(BF)
        table = np.block([[cosine, -sine], [sine, cosine]])
        pads.append(table)
        crops.append(table.T)
    return np.stack(pads), np.stack(crops)


def turn_polys():
    nodes = np.cos(np.pi * (np.arange(400) + 0.5) / 400) * 0.125 + 0.125
    root = np.sqrt(nodes)
    out = []
    for value in (np.cos(2 * np.pi * root), np.sin(2 * np.pi * root) / root):
        series = np.polynomial.chebyshev.Chebyshev.fit(nodes, value, 6, domain=[0, 0.25])
        out.append([float(c) for c in series.convert(kind=np.polynomial.Polynomial).coef])
    return out


COS_POLY, SIN_POLY = turn_polys()


def turn_pair(turns):
    square = turns * turns
    cosine = jnp.full_like(square, COS_POLY[-1])
    sine = jnp.full_like(square, SIN_POLY[-1])
    for c, s in zip(COS_POLY[-2::-1], SIN_POLY[-2::-1]):
        cosine = cosine * square + c
        sine = sine * square + s
    return cosine, sine * turns


def wrap(turns):
    return turns - jnp.floor(turns + 0.5)


def dot(left, right):
    return jnp.dot(left, right, preferred_element_type=F32)


def dot_nt(left, right):
    return lax.dot_general(left, right, (((1,), (1,)), ((), ())), preferred_element_type=F32)


def two(value):
    high = value.astype(BF)
    return high, (value - high.astype(F32)).astype(BF)


def spread(value, length):
    half = length // 2
    blank = jnp.zeros((value.shape[0], LANES - half), value.dtype)
    return jnp.concatenate([value[:, :half], blank, value[:, half:], blank], 1)


def table_rows(tx_ref, value):
    high, low = two(value)
    return dot(tx_ref[0], high) + dot(tx_ref[1], high) + dot(tx_ref[0], low)


def shear_rows(re, im, tx_ref, phase_ref, sign):
    width = re.shape[0]
    from_re, from_im = table_rows(tx_ref, re), table_rows(tx_ref, im)
    sr = from_re[:width] + from_im[width:]
    si = from_im[:width] - from_re[width:]
    c, s = phase_ref[0], phase_ref[1] * sign
    from_re, from_im = table_rows(tx_ref, sr * c - si * s), table_rows(tx_ref, sr * s + si * c)
    return from_re[:width] - from_im[width:], from_im[:width] + from_re[width:]


def shear_columns(re, im, ty_ref, phase_ref, sign):
    back = []
    for parity in range(2):
        join = (lambda v: v[:, :LANES] - v[:, LANES:]) if parity else (lambda v: v[:, :LANES] + v[:, LANES:])
        high, low = two(jnp.concatenate([join(re), join(im)], 1))
        th, tl = ty_ref[parity, 0], ty_ref[parity, 1]
        spectra = dot(high, th) + dot(low, th) + dot(high, tl)
        sr, si = spectra[:, :LANES], spectra[:, LANES:]
        c, s = phase_ref[2 * parity], phase_ref[2 * parity + 1] * sign
        high, low = two(jnp.concatenate([sr * c - si * s, sr * s + si * c], 1))
        back.append(dot_nt(high, th) + dot_nt(low, th) + dot_nt(high, tl))
    even, odd = back
    low_half, high_half = even + odd, even - odd
    return (
        jnp.concatenate([low_half[:, :LANES], high_half[:, :LANES]], 1),
        jnp.concatenate([low_half[:, LANES:], high_half[:, LANES:]], 1),
    )


def signed(counter, length):
    return jnp.where(counter < length // 2, counter, counter - length).astype(F32)


def make_phases(motion_ref, p1_ref, pc_ref, p3_ref, width, length):
    half = length // 2
    center = (LEVELS - 1) / 2.0
    shift_x = (motion_ref[0, 1].astype(F32) - center) * SHIFT_STEP
    shift_y = (motion_ref[0, 2].astype(F32) - center) * SHIFT_STEP
    angle = jnp.full((8, LANES), (motion_ref[0, 0].astype(F32) - center) * ANGLE_STEP, F32)
    tilt = jnp.sin(angle)[:1, :1]
    slope = -(jnp.sin(angle * 0.5) / jnp.cos(angle * 0.5))[:1, :1]
    lane = lax.broadcasted_iota(jnp.int32, (1, 2 * LANES), 1)
    line = jnp.where(lane < LANES, lane, lane - LANES + half)
    bend = slope * (line.astype(F32) - length / 2.0)
    freq = signed(lax.broadcasted_iota(jnp.int32, (width, 1), 0), width) * (-1.0 / width)
    for ref, shift in ((p1_ref, bend + shift_x), (p3_ref, bend)):
        c, s = turn_pair(wrap(freq * shift))
        ref[0] = c
        ref[1] = s
    along = lax.broadcasted_iota(jnp.int32, (width, 1), 0).astype(F32) - width / 2.0
    shift = tilt * along + shift_y
    lane = lax.broadcasted_iota(jnp.int32, (1, LANES), 1)
    for parity in range(2):
        freq = signed(2 * lane + parity, length) * (-1.0 / length)
        c, s = turn_pair(wrap(shift * freq))
        pc_ref[2 * parity] = c
        pc_ref[2 * parity + 1] = s


def make_projector(mask_ref, ty_ref, h_ref, length):
    half = length // 2
    mask = jnp.broadcast_to(mask_ref[...].astype(F32), (8, length)).astype(BF)
    line = lax.broadcasted_iota(jnp.int32, (length, 2 * LANES), 0)
    lane = lax.broadcasted_iota(jnp.int32, (length, 2 * LANES), 1) % LANES
    picked = []
    for parity in range(2):
        select = jnp.where((line == 2 * lane + parity) & (lane < half), 1.0, 0.0).astype(BF)
        picked.append(dot(mask, select)[:1])
    counts = [jnp.sum(p[:, :LANES], 1, keepdims=True) for p in picked]
    total = ((counts[0] + counts[1]) / length).astype(BF).astype(F32)
    larger = (jnp.maximum(counts[0], counts[1]) / length).astype(BF).astype(F32)
    rest = total - larger
    row = lax.broadcasted_iota(jnp.int32, (2 * LANES, 2 * LANES), 0)
    col = lax.broadcasted_iota(jnp.int32, (2 * LANES, 2 * LANES), 1)
    diagonal = (row == col) & (row % LANES < half)
    for parity in range(2):
        th, tl = ty_ref[parity, 0], ty_ref[parity, 1]
        keep = picked[parity]
        mh = (th.astype(F32) * keep).astype(BF)
        ml = (tl.astype(F32) * keep).astype(BF)
        table = dot_nt(mh, th) + dot_nt(ml, th) + dot_nt(mh, tl)
        value = jnp.where(counts[parity] >= counts[1 - parity], larger, rest)
        if parity:
            value = jnp.where(counts[1] > counts[0], larger, rest)
        h_ref[parity] = jnp.where(diagonal, value, table).astype(BF)


def make_wave(psf_ref, psft_ref, wave_ref, length, classes):
    half = length // 2
    readout = psf_ref.shape[1]
    blank = jnp.zeros((LANES - half, readout), F32)
    psf = jnp.concatenate([psf_ref[:half], blank, psf_ref[half:], blank], 0) * (0.5 / np.pi)
    wide = -(-readout // LANES) * LANES
    if wide > readout:
        psf = jnp.concatenate([psf, jnp.zeros((2 * LANES, wide - readout), F32)], 1)
    for side in range(2):
        psft_ref[side] = psf[side * LANES:(side + 1) * LANES].T
    rows = readout // classes
    for j in range(classes):
        picked = pl.ds(j, rows, stride=classes)
        c, s = turn_pair(jnp.concatenate([psft_ref[0, picked, :], psft_ref[1, picked, :]], 1))
        wave_ref[0, j] = c
        wave_ref[1, j] = s


def one_coil(coil, rot_ref, acc_ref, pt_ref, ct_ref, wave_ref, h_ref, w_ref, length, classes):
    width = rot_ref.shape[1]
    half = width // 2
    cr = spread(coil[0], length).astype(F32)
    ci = spread(coil[1], length).astype(F32)
    rr, ri = rot_ref[0], rot_ref[1]
    zr = cr * rr - ci * ri
    zi = cr * ri + ci * rr
    ar, ai, br, bi = zr[:half], zi[:half], zr[half:], zi[half:]
    for j in range(classes // 2):
        angle = -2 * np.pi * j / classes
        wr, wi = float(np.cos(angle)), float(np.sin(angle))
        if j == 0:
            ur, ui = br, bi
        else:
            ur, ui = br * wr - bi * wi, br * wi + bi * wr
        for step in range(2):
            cls = j + step * (classes // 2)
            tr, ti = (ar - ur, ai - ui) if step else (ar + ur, ai + ui)
            spectra = dot(pt_ref[cls], jnp.concatenate([tr, ti], 0).astype(BF))
            sr, si = spectra[:half], spectra[half:]
            c, s = wave_ref[0, cls], wave_ref[1, cls]
            vr = sr * c - si * s
            vi = sr * s + si * c
            rows = pl.ds(cls * half, half)
            w_ref[0, rows, :LANES] = (vr[:, :LANES] + vr[:, LANES:]).astype(BF)
            w_ref[0, rows, LANES:] = (vi[:, :LANES] + vi[:, LANES:]).astype(BF)
            w_ref[1, rows, :LANES] = (vr[:, :LANES] - vr[:, LANES:]).astype(BF)
            w_ref[1, rows, LANES:] = (vi[:, :LANES] - vi[:, LANES:]).astype(BF)
    back0 = back1 = None
    for j in range(classes // 2):
        pair = []
        for step in range(2):
            cls = j + step * (classes // 2)
            rows = pl.ds(cls * half, half)
            plus = dot(w_ref[0, rows, :], h_ref[0])
            minus = dot(w_ref[1, rows, :], h_ref[1])
            low, high = plus + minus, plus - minus
            yr = jnp.concatenate([low[:, :LANES], high[:, :LANES]], 1)
            yi = jnp.concatenate([low[:, LANES:], high[:, LANES:]], 1)
            c, s = wave_ref[0, cls], wave_ref[1, cls]
            ur = yr * c + yi * s
            ui = yi * c - yr * s
            pair.append(dot(ct_ref[cls], jnp.concatenate([ur, ui], 0).astype(BF)))
        total, diff = pair[0] + pair[1], pair[0] - pair[1]
        angle = 2 * np.pi * j / classes
        wr, wi = float(np.cos(angle)), float(np.sin(angle))
        dr, di = diff[:half], diff[half:]
        if j == 0:
            back0, back1 = total, [dr, di]
        else:
            back0 = back0 + total
            back1 = [back1[0] + (dr * wr - di * wi), back1[1] + (dr * wi + di * wr)]
    backr = jnp.concatenate([back0[:half], back1[0]], 0)
    backi = jnp.concatenate([back0[half:], back1[1]], 0)
    acc_ref[0] += cr * backr + ci * backi
    acc_ref[1] += cr * backi - ci * backr


def kernel(
    motion_ref, mask_ref, image_ref, psf_ref, coil_ref, pt_ref, ct_ref, tx_ref, ty_ref, out_ref,
    rot_ref, acc_ref, p1_ref, pc_ref, p3_ref, psft_ref, wave_ref, h_ref, w_ref, *, length, classes,
):
    step = pl.program_id(0)
    width = rot_ref.shape[1]
    half = length // 2

    @pl.when(step == 0)
    def _():
        make_phases(motion_ref, p1_ref, pc_ref, p3_ref, width, length)
        re, im = spread(image_ref[0], length), spread(image_ref[1], length)
        re, im = shear_rows(re, im, tx_ref, p1_ref, 1.0)
        re, im = shear_columns(re, im, ty_ref, pc_ref, 1.0)
        re, im = shear_rows(re, im, tx_ref, p3_ref, 1.0)
        rot_ref[0] = re
        rot_ref[1] = im
        acc_ref[...] = jnp.zeros_like(acc_ref)
        make_projector(mask_ref, ty_ref, h_ref, length)
        make_wave(psf_ref, psft_ref, wave_ref, length, classes)

    for c in range(coil_ref.shape[0]):
        one_coil(coil_ref[c], rot_ref, acc_ref, pt_ref, ct_ref, wave_ref, h_ref, w_ref.at[c], length, classes)

    @pl.when(step == pl.num_programs(0) - 1)
    def _():
        re, im = acc_ref[0], acc_ref[1]
        re, im = shear_rows(re, im, tx_ref, p3_ref, -1.0)
        re, im = shear_columns(re, im, ty_ref, pc_ref, -1.0)
        re, im = shear_rows(re, im, tx_ref, p1_ref, -1.0)
        for part, value in enumerate((re, im)):
            out_ref[part] = jnp.concatenate([value[:, :half], value[:, LANES:LANES + half]], 1)


def slice_operator(motion, mask, image, psf, coils):
    _, width, length = image.shape
    readout = psf.shape[1]
    count = coils.shape[0]
    classes = readout // (width // 2)
    pads, crops = readout_tables(width, readout)
    tx, ty = row_tables(width), column_tables(length)
    per_step = 2 if count % 2 == 0 else 1
    whole = lambda shape: pl.BlockSpec(shape, lambda i: (0,) * len(shape))
    wide = -(-readout // LANES) * LANES
    return pl.pallas_call(
        functools.partial(kernel, length=length, classes=classes),
        grid=(count // per_step,),
        in_specs=[
            pl.BlockSpec(memory_space=pltpu.SMEM),
            whole(mask.shape),
            whole(image.shape),
            whole(psf.shape),
            pl.BlockSpec((per_step, 2, width, length), lambda i: (i, 0, 0, 0)),
            whole(pads.shape),
            whole(crops.shape),
            whole(tx.shape),
            whole(ty.shape),
        ],
        out_specs=whole(image.shape),
        out_shape=jax.ShapeDtypeStruct(image.shape, F32),
        scratch_shapes=[
            pltpu.VMEM((2, width, 2 * LANES), F32),
            pltpu.VMEM((2, width, 2 * LANES), F32),
            pltpu.VMEM((2, width, 2 * LANES), F32),
            pltpu.VMEM((4, width, LANES), F32),
            pltpu.VMEM((2, width, 2 * LANES), F32),
            pltpu.VMEM((2, wide, LANES), F32),
            pltpu.VMEM((2, classes, width // 2, 2 * LANES), F32),
            pltpu.VMEM((2, 2 * LANES, 2 * LANES), BF),
            pltpu.VMEM((per_step, 2, readout, 2 * LANES), BF),
        ],
        compiler_params=pltpu.CompilerParams(vmem_limit_bytes=48 * 2**20),
        name="normal_operator",
    )(motion, mask, image, psf, coils, jnp.asarray(pads), jnp.asarray(crops), jnp.asarray(tx), jnp.asarray(ty))


def from_partner(value, axis, apart):
    mask = 2**apart
    pairs = [(source, source ^ mask) for source in range(lax.axis_size(axis))]
    return lax.ppermute(value, axis, pairs)


def gather_slice(values, bit_count, device_rank):
    for bit_index in range(bit_count):
        partner = from_partner(values, "space", bit_index)
        low_side = device_rank >> bit_index & 1 == 0
        values = jnp.where(
            low_side, jnp.concatenate([values, partner], 0), jnp.concatenate([partner, values], 0)
        )
    return values


def sum_slice(values, bit_count, device_rank):
    for bit_index in reversed(range(bit_count)):
        half_rows = values.shape[0] // 2
        low_side = device_rank >> bit_index & 1 == 0
        kept_part = jnp.where(low_side, values[:half_rows], values[half_rows:])
        sent_part = jnp.where(low_side, values[half_rows:], values[:half_rows])
        values = kept_part + from_partner(sent_part, "space", bit_index)
    return values


def regroup_coils(coil_maps, bit_count, device_rank):
    group_size = 1 << bit_count
    pieces = coil_maps.reshape((group_size, coil_maps.shape[0] // group_size) + coil_maps.shape[1:])
    for bit_index in range(bit_count):
        old_shape = pieces.shape
        halves = pieces.reshape((group_size >> bit_index + 1, 2, 1 << bit_index) + old_shape[1:])
        low_side = device_rank >> bit_index & 1 == 0
        kept_part = jnp.where(low_side, halves[:, 0], halves[:, 1])
        sent_part = jnp.where(low_side, halves[:, 1], halves[:, 0])
        partner = from_partner(sent_part, "space", bit_index)
        pieces = jnp.stack(
            [jnp.where(low_side, kept_part, partner), jnp.where(low_side, partner, kept_part)], 1
        ).reshape(old_shape)
    moved = jnp.moveaxis(pieces, 0, 1)
    return moved.reshape((moved.shape[0], group_size * coil_maps.shape[1]) + coil_maps.shape[2:])


def on_device(image, coil_maps, psf_phase, line_mask, motion):
    lines = image.shape[0]
    length = line_mask.shape[1]
    device_rank = lax.axis_index("space")
    group_size = max(1, length // lines)
    bit_count = group_size.bit_length() - 1
    if bit_count:
        coil_maps = regroup_coils(coil_maps, bit_count, device_rank)
        psf_phase = gather_slice(psf_phase, bit_count, device_rank)
        image = gather_slice(image, bit_count, device_rank)
    image = jnp.transpose(image, (1, 2, 0))
    coil_maps = jnp.transpose(coil_maps, (0, 2, 3, 1))
    results = []
    for start in range(0, image.shape[2], length):
        stop = start + length
        results.append(
            slice_operator(
                motion, line_mask, image[:, :, start:stop], psf_phase[start:stop], coil_maps[..., start:stop]
            )
        )
    result = results[0] if len(results) == 1 else jnp.concatenate(results, 2)
    if bit_count:
        result = jnp.transpose(result, (2, 0, 1))
        result = sum_slice(result, bit_count, device_rank)
        result = jnp.transpose(result, (1, 2, 0))
    shots = lax.axis_size("shot")
    total = result
    for apart in range(1, shots):
        pairs = [(source, (source + apart) % shots) for source in range(shots)]
        total = total + lax.ppermute(result, "shot", pairs)
    return jnp.transpose(total, (2, 0, 1))


def solution(mesh):
    in_specs = (
        P(("parts", "space"), None, None),
        P(None, ("parts", "space"), None, None),
        P(("parts", "space"), None),
        P(("parts", "shot"), None),
        P(("parts", "shot"), None),
    )
    out_specs = P(("parts", "space"), None, None)
    return jax.shard_map(
        on_device, mesh=mesh, in_specs=in_specs, out_specs=out_specs, check_vma=False
    )
```

profile of v0, /device:TPU:13, one launch (start us, length us, event | category | flops | bytes accessed | tf_op | source)
XLA Modules:
  0.0 47.4 jit_solution(8769192068712408010)
XLA Ops:
  0.0 0.0 copy-start
  0.0 1.1 %copy-done = bf16[6,192,192]{2,1,0:T(8,128)(2,1)S(1)} copy-done((bf16[6,192,192]{2,1,0:T(8,128)(2,1)S(1)}, bf16[6,192,192]{2,1,0:T(8,128)(2,1)}, u32[]{:S(2)}) %copy-start) | copy-done | bytes 442392
  1.1 0.0 copy-start.1
  1.1 1.1 %copy-done.1 = bf16[6,192,192]{2,1,0:T(8,128)(2,1)S(1)} copy-done((bf16[6,192,192]{2,1,0:T(8,128)(2,1)S(1)}, bf16[6,192,192]{2,1,0:T(8,128)(2,1)}, u32[]{:S(2)}) %copy-start.1) | copy-done | bytes 442392
  2.1 0.0 copy-start.2
  2.1 1.0 %copy-done.2 = bf16[2,2,256,256]{3,2,1,0:T(8,128)(2,1)S(1)} copy-done((bf16[2,2,256,256]{3,2,1,0:T(8,128)(2,1)S(1)}, bf16[2,2,256,256]{3,2,1,0:T(8,128)(2,1)}, u32[]{:S(2)}) %copy-start.2) | copy-done | bytes 524312
  3.2 0.0 copy-start.3
  3.2 1.0 %copy-done.3 = f32[200,576]{1,0:T(8,128)S(1)} copy-done((f32[200,576]{1,0:T(8,128)S(1)}, f32[200,576]{1,0:T(8,128)}, u32[]{:S(2)}) %copy-start.3) | copy-done | bytes 460824
  4.2 0.0 copy-start.4
  4.2 1.0 %copy-done.4 = f32[200,2,192]{0,2,1:T(8,128)S(1)} copy-done((f32[200,2,192]{0,2,1:T(8,128)S(1)}, f32[200,2,192]{0,2,1:T(8,128)}, u32[]{:S(2)}) %copy-start.4) | copy-done | bytes 307224
  5.2 0.0 copy-start.5
  5.2 1.0 %copy-done.5 = bf16[2,384,192]{2,1,0:T(8,128)(2,1)S(1)} copy-done((bf16[2,384,192]{2,1,0:T(8,128)(2,1)S(1)}, bf16[2,384,192]{2,1,0:T(8,128)(2,1)}, u32[]{:S(2)}) %copy-start.5) | copy-done | bytes 294936
  6.2 0.0 copy-start.6
  6.2 0.7 %copy-done.6 = s32[1,200]{1,0:T(1,128)S(1)} copy-done((s32[1,200]{1,0:T(1,128)S(1)}, s32[1,200]{1,0:T(1,128)}, u32[]{:S(2)}) %copy-start.6) | copy-done | bytes 824
  6.9 0.0 copy-start.7
  6.9 0.7 %copy-done.7 = s32[1,3]{1,0:T(1,128)S(1)} copy-done((s32[1,3]{1,0:T(1,128)S(1)}, s32[1,3]{1,0:T(1,128)}, u32[]{:S(2)}) %copy-start.7) | copy-done | bytes 36
  7.5 37.0 %normal_operator.1 = f32[2,192,200]{2,1,0:T(8,128)S(1)} custom-call(s32[1,3]{1,0:T(1,128)S(1)} %copy-done.7, s32[1,200]{1,0:T(1,128)S(1)} %copy-done.6, f32[2,192,200]{2,1,0:T(8,128)S(1)} %bitcast.4, f32[200,576]{1,0:T(8,128)S(1)} %copy-done.3, bf16[16,2,192,200]{3,2,1,0:T(8,128)(2,1)} %bitcast.5, bf16[6,192,192]{2,1,0:T(8,128)(2,1)S(1)} %copy-done.1, ...), custom_call_target="tpu_custom_call" | custom-call | tf_op jit(solution)/shard_map/normal_operator/pallas_call | solution.py:323
  44.5 0.7 %collective-permute-start = (f32[2,192,200]{2,1,0:T(8,128)S(1)}, f32[2,192,200]{2,1,0:T(8,128)S(1)}, u32[]{:S(2)}, u32[]{:S(2)}) collective-permute-start(f32[2,192,200]{2,1,0:T(8,128)S(1)} %normal_operator.1), channel_id=1, source_target_pairs={{0,8},{8,0},{1,9},{9,1},{2,10},{10,2},{3,11},{11,3},{4,12},{12,4},... | collective-permute-start | bytes 921608 | tf_op jit(solution)/shard_map/ppermute | solution.py:427
  45.3 1.3 %collective-permute-done = f32[2,192,200]{2,1,0:T(8,128)S(1)} collective-permute-done((f32[2,192,200]{2,1,0:T(8,128)S(1)}, f32[2,192,200]{2,1,0:T(8,128)S(1)}, u32[]{:S(2)}, u32[]{:S(2)}) %collective-permute-start) | collective-permute-done | bytes 307232 | tf_op jit(solution)/shard_map/ppermute | solution.py:427
  46.6 0.8 %add_bitcast_fusion = f32[200,2,192]{0,2,1:T(8,128)} fusion(f32[2,192,200]{2,1,0:T(8,128)S(1)} %normal_operator.1, f32[2,192,200]{2,1,0:T(8,128)S(1)} %collective-permute-done), kind=kLoop, calls=%fused_computation | loop fusion | flops 76800 | bytes 921600 | tf_op jit(solution)/shard_map/transpose | solution.py:428
Async XLA Ops:
  0.0 1.1 %copy-start = (bf16[6,192,192]{2,1,0:T(8,128)(2,1)S(1)}, bf16[6,192,192]{2,1,0:T(8,128)(2,1)}, u32[]{:S(2)}) copy-start(bf16[6,192,192]{2,1,0:T(8,128)(2,1)} %constant.9.clone.ct_ref) | copy-start | bytes 1327108
  1.1 1.1 %copy-start.1 = (bf16[6,192,192]{2,1,0:T(8,128)(2,1)S(1)}, bf16[6,192,192]{2,1,0:T(8,128)(2,1)}, u32[]{:S(2)}) copy-start(bf16[6,192,192]{2,1,0:T(8,128)(2,1)} %constant.8.clone.pt_ref) | copy-start | bytes 1327108
  2.1 1.0 %copy-start.2 = (bf16[2,2,256,256]{3,2,1,0:T(8,128)(2,1)S(1)}, bf16[2,2,256,256]{3,2,1,0:T(8,128)(2,1)}, u32[]{:S(2)}) copy-start(bf16[2,2,256,256]{3,2,1,0:T(8,128)(2,1)} %constant.11.clone.ty_ref) | copy-start | bytes 1572868
  3.2 1.0 %copy-start.3 = (f32[200,576]{1,0:T(8,128)S(1)}, f32[200,576]{1,0:T(8,128)}, u32[]{:S(2)}) copy-start(f32[200,576]{1,0:T(8,128)} %psf_ref.1) | copy-start | bytes 1382404
  4.2 1.0 %copy-start.4 = (f32[200,2,192]{0,2,1:T(8,128)S(1)}, f32[200,2,192]{0,2,1:T(8,128)}, u32[]{:S(2)}) copy-start(f32[200,2,192]{0,2,1:T(8,128)} %param.9) | copy-start | bytes 921604
  5.2 1.0 %copy-start.5 = (bf16[2,384,192]{2,1,0:T(8,128)(2,1)S(1)}, bf16[2,384,192]{2,1,0:T(8,128)(2,1)}, u32[]{:S(2)}) copy-start(bf16[2,384,192]{2,1,0:T(8,128)(2,1)} %constant.10.clone.tx_ref) | copy-start | bytes 884740
  6.2 0.7 %copy-start.6 = (s32[1,200]{1,0:T(1,128)S(1)}, s32[1,200]{1,0:T(1,128)}, u32[]{:S(2)}) copy-start(s32[1,200]{1,0:T(1,128)} %mask_ref.1) | copy-start | bytes 2404
  6.9 0.7 %copy-start.7 = (s32[1,3]{1,0:T(1,128)S(1)}, s32[1,3]{1,0:T(1,128)}, u32[]{:S(2)}) copy-start(s32[1,3]{1,0:T(1,128)} %motion_ref.1) | copy-start | bytes 40
  44.5 2.1 %collective-permute-start = (f32[2,192,200]{2,1,0:T(8,128)S(1)}, f32[2,192,200]{2,1,0:T(8,128)S(1)}, u32[]{:S(2)}, u32[]{:S(2)}) collective-permute-start(f32[2,192,200]{2,1,0:T(8,128)S(1)} %normal_operator.1), channel_id=1, source_target_pairs={{0,8},{8,0},{1,9},{9,1},{2,10},{10,2},{3,11},{11,3},{4,12},{12,4},... | collective-permute-start | bytes 921608 | tf_op jit(solution)/shard_map/ppermute | solution.py:427
where the time goes:
time: 47.9 us; the launch traced here: 47.4 us
  Pallas kernels  37 us (77%)
  local copies, waits for them, and re-layouts  7.53 us (16%)
  waiting for transfers between devices  1.35 us (3%)
  other arithmetic  0.82 us (2%)
  starting transfers between devices  0.74 us (2%)
    pallas_call x1, Pallas kernels, slice_operator(): pl.pallas_call(functools.partial(kernel, length=length, classes=classes),...  37 us
    unnamed x16, local copies, waits for them, and re-layouts  7.53 us
    ppermute x1, waiting for transfers between devices, on_device(): total = total + lax.ppermute(result, 'shot', pairs)  1.35 us
  transfers between devices with their start and end apart: 1, of which 1 were waited for; matrix products, arithmetic and copies ran while one was open for 0% of the time, Pallas kernels for 0%

commit v1 on v0

--- a/solution.py
+++ b/solution.py
@@ -51,14 +51,13 @@
     pads, crops = [], []
     for j in range(classes):
         k = np.arange(half)[:, None] * classes + j
-        x = np.arange(half)[None, :]
+        x = np.arange(width)[None, :]
         angle = -2 * np.pi * (k * x % readout) / readout
         cosine = (np.cos(angle) / np.sqrt(readout)).astype(np.float32).astype(BF)
         sine = (np.sin(angle) / np.sqrt(readout)).astype(np.float32).astype(BF)
-        table = np.block([[cosine, -sine], [sine, cosine]])
-        pads.append(table)
-        crops.append(table.T)
-    return np.stack(pads), np.stack(crops)
+        pads.append(np.block([[cosine[:, :half], -sine[:, :half]], [sine[:, :half], cosine[:, :half]]]))
+        crops.append(np.block([[cosine.T, sine.T], [-sine.T, cosine.T]]))
+    return np.stack(pads), np.concatenate(crops, 1)
 
 
 def turn_polys():
@@ -117,12 +116,13 @@
     from_re, from_im = table_rows(tx_ref, re), table_rows(tx_ref, im)
     sr = from_re[:width] + from_im[width:]
     si = from_im[:width] - from_re[width:]
-    c, s = phase_ref[0], phase_ref[1] * sign
+    c, s = phase_ref[0, :width], phase_ref[1, :width] * sign
     from_re, from_im = table_rows(tx_ref, sr * c - si * s), table_rows(tx_ref, sr * s + si * c)
     return from_re[:width] - from_im[width:], from_im[:width] + from_re[width:]
 
 
 def shear_columns(re, im, ty_ref, phase_ref, sign):
+    width = re.shape[0]
     back = []
     for parity in range(2):
         join = (lambda v: v[:, :LANES] - v[:, LANES:]) if parity else (lambda v: v[:, :LANES] + v[:, LANES:])
@@ -130,7 +130,7 @@
         th, tl = ty_ref[parity, 0], ty_ref[parity, 1]
         spectra = dot(high, th) + dot(low, th) + dot(high, tl)
         sr, si = spectra[:, :LANES], spectra[:, LANES:]
-        c, s = phase_ref[2 * parity], phase_ref[2 * parity + 1] * sign
+        c, s = phase_ref[parity, 0, :width], phase_ref[parity, 1, :width] * sign
         high, low = two(jnp.concatenate([sr * c - si * s, sr * s + si * c], 1))
         back.append(dot_nt(high, th) + dot_nt(low, th) + dot_nt(high, tl))
     even, odd = back
@@ -143,6 +143,11 @@
 
 def signed(counter, length):
     return jnp.where(counter < length // 2, counter, counter - length).astype(F32)
+
+
+def put(ref, re, im):
+    ref[0, :re.shape[0]] = re
+    ref[1, :im.shape[0]] = im
 
 
 def make_phases(motion_ref, p1_ref, pc_ref, p3_ref, width, length):
@@ -157,18 +162,17 @@
     line = jnp.where(lane < LANES, lane, lane - LANES + half)
     bend = slope * (line.astype(F32) - length / 2.0)
     freq = signed(lax.broadcasted_iota(jnp.int32, (width, 1), 0), width) * (-1.0 / width)
-    for ref, shift in ((p1_ref, bend + shift_x), (p3_ref, bend)):
-        c, s = turn_pair(wrap(freq * shift))
-        ref[0] = c
-        ref[1] = s
+    c, s = turn_pair(wrap(freq * bend))
+    put(p3_ref, c, s)
+    cx, sx = turn_pair(wrap(freq * shift_x))
+    put(p1_ref, c * cx - s * sx, c * sx + s * cx)
     along = lax.broadcasted_iota(jnp.int32, (width, 1), 0).astype(F32) - width / 2.0
     shift = tilt * along + shift_y
     lane = lax.broadcasted_iota(jnp.int32, (1, LANES), 1)
     for parity in range(2):
         freq = signed(2 * lane + parity, length) * (-1.0 / length)
         c, s = turn_pair(wrap(shift * freq))
-        pc_ref[2 * parity] = c
-        pc_ref[2 * parity + 1] = s
+        put(pc_ref.at[parity], c, s)
 
 
 def make_projector(mask_ref, ty_ref, h_ref, length):
@@ -213,18 +217,17 @@
     for j in range(classes):
         picked = pl.ds(j, rows, stride=classes)
         c, s = turn_pair(jnp.concatenate([psft_ref[0, picked, :], psft_ref[1, picked, :]], 1))
-        wave_ref[0, j] = c
-        wave_ref[1, j] = s
-
-
-def one_coil(coil, rot_ref, acc_ref, pt_ref, ct_ref, wave_ref, h_ref, w_ref, length, classes):
-    width = rot_ref.shape[1]
+        put(wave_ref.at[j], c.astype(BF), s.astype(BF))
+
+
+def one_coil(coil, rot_ref, acc_ref, pt_ref, ct_ref, wave_ref, h_ref, w_ref, u_ref, length, classes):
+    width = coil.shape[1]
     half = width // 2
-    cr = spread(coil[0], length).astype(F32)
-    ci = spread(coil[1], length).astype(F32)
-    rr, ri = rot_ref[0], rot_ref[1]
-    zr = cr * rr - ci * ri
-    zi = cr * ri + ci * rr
+    cr = spread(coil[0], length)
+    ci = spread(coil[1], length)
+    rr, ri = rot_ref[0, :width], rot_ref[1, :width]
+    zr = (cr.astype(F32) * rr - ci.astype(F32) * ri).astype(BF)
+    zi = (cr.astype(F32) * ri + ci.astype(F32) * rr).astype(BF)
     ar, ai, br, bi = zr[:half], zi[:half], zr[half:], zi[half:]
     for j in range(classes // 2):
         angle = -2 * np.pi * j / classes
@@ -236,78 +239,77 @@
         for step in range(2):
             cls = j + step * (classes // 2)
             tr, ti = (ar - ur, ai - ui) if step else (ar + ur, ai + ui)
-            spectra = dot(pt_ref[cls], jnp.concatenate([tr, ti], 0).astype(BF))
+            spectra = dot(pt_ref[cls], jnp.concatenate([tr, ti], 0)).astype(BF)
             sr, si = spectra[:half], spectra[half:]
-            c, s = wave_ref[0, cls], wave_ref[1, cls]
+            c, s = wave_ref[cls, 0, :half], wave_ref[cls, 1, :half]
             vr = sr * c - si * s
             vi = sr * s + si * c
             rows = pl.ds(cls * half, half)
-            w_ref[0, rows, :LANES] = (vr[:, :LANES] + vr[:, LANES:]).astype(BF)
-            w_ref[0, rows, LANES:] = (vi[:, :LANES] + vi[:, LANES:]).astype(BF)
-            w_ref[1, rows, :LANES] = (vr[:, :LANES] - vr[:, LANES:]).astype(BF)
-            w_ref[1, rows, LANES:] = (vi[:, :LANES] - vi[:, LANES:]).astype(BF)
-    back0 = back1 = None
-    for j in range(classes // 2):
-        pair = []
-        for step in range(2):
-            cls = j + step * (classes // 2)
-            rows = pl.ds(cls * half, half)
-            plus = dot(w_ref[0, rows, :], h_ref[0])
-            minus = dot(w_ref[1, rows, :], h_ref[1])
-            low, high = plus + minus, plus - minus
-            yr = jnp.concatenate([low[:, :LANES], high[:, :LANES]], 1)
-            yi = jnp.concatenate([low[:, LANES:], high[:, LANES:]], 1)
-            c, s = wave_ref[0, cls], wave_ref[1, cls]
-            ur = yr * c + yi * s
-            ui = yi * c - yr * s
-            pair.append(dot(ct_ref[cls], jnp.concatenate([ur, ui], 0).astype(BF)))
-        total, diff = pair[0] + pair[1], pair[0] - pair[1]
-        angle = 2 * np.pi * j / classes
-        wr, wi = float(np.cos(angle)), float(np.sin(angle))
-        dr, di = diff[:half], diff[half:]
-        if j == 0:
-            back0, back1 = total, [dr, di]
-        else:
-            back0 = back0 + total
-            back1 = [back1[0] + (dr * wr - di * wi), back1[1] + (dr * wi + di * wr)]
-    backr = jnp.concatenate([back0[:half], back1[0]], 0)
-    backi = jnp.concatenate([back0[half:], back1[1]], 0)
-    acc_ref[0] += cr * backr + ci * backi
-    acc_ref[1] += cr * backi - ci * backr
+            w_ref[0, rows, :LANES] = vr[:, :LANES] + vr[:, LANES:]
+            w_ref[0, rows, LANES:] = vi[:, :LANES] + vi[:, LANES:]
+            w_ref[1, rows, :LANES] = vr[:, :LANES] - vr[:, LANES:]
+            w_ref[1, rows, LANES:] = vi[:, :LANES] - vi[:, LANES:]
+    readout = classes * half
+    plus = dot(w_ref[0, :readout], h_ref[0]).astype(BF)
+    minus = dot(w_ref[1, :readout], h_ref[1]).astype(BF)
+    for cls in range(classes):
+        rows = slice(cls * half, (cls + 1) * half)
+        for side, y in enumerate((plus[rows] + minus[rows], plus[rows] - minus[rows])):
+            lanes = slice(side * LANES, (side + 1) * LANES)
+            yr, yi = y[:, :LANES], y[:, LANES:]
+            c, s = wave_ref[cls, 0, :half, lanes], wave_ref[cls, 1, :half, lanes]
+            u_ref[pl.ds(2 * cls * half, half), lanes] = yr * c + yi * s
+            u_ref[pl.ds((2 * cls + 1) * half, half), lanes] = yi * c - yr * s
+    back = dot(ct_ref[...], u_ref[...])
+    br, bi = back[:width], back[width:]
+    crf, cif = cr.astype(F32), ci.astype(F32)
+    acc_ref[0, :width] += crf * br + cif * bi
+    acc_ref[1, :width] += crf * bi - cif * br
 
 
 def kernel(
-    motion_ref, mask_ref, image_ref, psf_ref, coil_ref, pt_ref, ct_ref, tx_ref, ty_ref, out_ref,
-    rot_ref, acc_ref, p1_ref, pc_ref, p3_ref, psft_ref, wave_ref, h_ref, w_ref, *, length, classes,
+    motion_hbm, mask_hbm, image_hbm, tx_hbm, ty_hbm, psf_hbm, pt_hbm, coil_hbm, ct_hbm, out_ref,
+    motion_ref, mask_ref, image_ref, tx_ref, ty_ref, psf_ref, pt_ref, coil_ref, ct_ref,
+    rot_ref, acc_ref, p1_ref, pc_ref, p3_ref, psft_ref, wave_ref, h_ref, w_ref, u_ref, sems,
+    *, length, classes, per_step,
 ):
-    step = pl.program_id(0)
-    width = rot_ref.shape[1]
-    half = length // 2
-
-    @pl.when(step == 0)
-    def _():
-        make_phases(motion_ref, p1_ref, pc_ref, p3_ref, width, length)
-        re, im = spread(image_ref[0], length), spread(image_ref[1], length)
-        re, im = shear_rows(re, im, tx_ref, p1_ref, 1.0)
-        re, im = shear_columns(re, im, ty_ref, pc_ref, 1.0)
-        re, im = shear_rows(re, im, tx_ref, p3_ref, 1.0)
-        rot_ref[0] = re
-        rot_ref[1] = im
-        acc_ref[...] = jnp.zeros_like(acc_ref)
-        make_projector(mask_ref, ty_ref, h_ref, length)
-        make_wave(psf_ref, psft_ref, wave_ref, length, classes)
-
-    for c in range(coil_ref.shape[0]):
-        one_coil(coil_ref[c], rot_ref, acc_ref, pt_ref, ct_ref, wave_ref, h_ref, w_ref.at[c], length, classes)
-
-    @pl.when(step == pl.num_programs(0) - 1)
-    def _():
-        re, im = acc_ref[0], acc_ref[1]
-        re, im = shear_rows(re, im, tx_ref, p3_ref, -1.0)
-        re, im = shear_columns(re, im, ty_ref, pc_ref, -1.0)
-        re, im = shear_rows(re, im, tx_ref, p1_ref, -1.0)
-        for part, value in enumerate((re, im)):
-            out_ref[part] = jnp.concatenate([value[:, :half], value[:, LANES:LANES + half]], 1)
+    width = image_ref.shape[1]
+    half = length // 2
+    sources = (motion_hbm, mask_hbm, image_hbm, tx_hbm, ty_hbm, psf_hbm, pt_hbm, coil_hbm, ct_hbm)
+    targets = (motion_ref, mask_ref, image_ref, tx_ref, ty_ref, psf_ref, pt_ref, coil_ref, ct_ref)
+    copies = [pltpu.make_async_copy(a, b, sems.at[i]) for i, (a, b) in enumerate(zip(sources, targets))]
+    for copy in copies:
+        copy.start()
+    for copy in copies[:6]:
+        copy.wait()
+    make_phases(motion_ref, p1_ref, pc_ref, p3_ref, width, length)
+    re, im = spread(image_ref[0], length), spread(image_ref[1], length)
+    re, im = shear_rows(re, im, tx_ref, p1_ref, 1.0)
+    re, im = shear_columns(re, im, ty_ref, pc_ref, 1.0)
+    re, im = shear_rows(re, im, tx_ref, p3_ref, 1.0)
+    put(rot_ref, re, im)
+    acc_ref[...] = jnp.zeros_like(acc_ref)
+    make_projector(mask_ref, ty_ref, h_ref, length)
+    make_wave(psf_ref, psft_ref, wave_ref, length, classes)
+    for copy in copies[6:]:
+        copy.wait()
+
+    def some_coils(step, carry):
+        for c in range(per_step):
+            one_coil(
+                coil_ref[step * per_step + c], rot_ref, acc_ref, pt_ref, ct_ref, wave_ref, h_ref,
+                w_ref.at[c], u_ref.at[c], length, classes,
+            )
+        return carry
+
+    lax.fori_loop(0, coil_ref.shape[0] // per_step, some_coils, 0)
+
+    re, im = acc_ref[0, :width], acc_ref[1, :width]
+    re, im = shear_rows(re, im, tx_ref, p3_ref, -1.0)
+    re, im = shear_columns(re, im, ty_ref, pc_ref, -1.0)
+    re, im = shear_rows(re, im, tx_ref, p1_ref, -1.0)
+    for part, value in enumerate((re, im)):
+        out_ref[part] = jnp.concatenate([value[:, :half], value[:, LANES:LANES + half]], 1)
 
 
 def slice_operator(motion, mask, image, psf, coils):
@@ -318,38 +320,31 @@
     pads, crops = readout_tables(width, readout)
     tx, ty = row_tables(width), column_tables(length)
     per_step = 2 if count % 2 == 0 else 1
-    whole = lambda shape: pl.BlockSpec(shape, lambda i: (0,) * len(shape))
     wide = -(-readout // LANES) * LANES
+    operands = (motion, mask, image, jnp.asarray(tx), jnp.asarray(ty), psf, jnp.asarray(pads), coils, jnp.asarray(crops))
     return pl.pallas_call(
-        functools.partial(kernel, length=length, classes=classes),
-        grid=(count // per_step,),
-        in_specs=[
-            pl.BlockSpec(memory_space=pltpu.SMEM),
-            whole(mask.shape),
-            whole(image.shape),
-            whole(psf.shape),
-            pl.BlockSpec((per_step, 2, width, length), lambda i: (i, 0, 0, 0)),
-            whole(pads.shape),
-            whole(crops.shape),
-            whole(tx.shape),
-            whole(ty.shape),
+        functools.partial(kernel, length=length, classes=classes, per_step=per_step),
+        in_specs=[pl.BlockSpec(memory_space=pltpu.HBM) for _ in operands],
+        out_specs=pl.BlockSpec(memory_space=pltpu.VMEM),
+        out_shape=jax.ShapeDtypeStruct(image.shape, F32),
+        scratch_shapes=[pltpu.SMEM(motion.shape, motion.dtype)]
+        + [pltpu.VMEM(a.shape, a.dtype) for a in operands[1:]]
+        + [
+            pltpu.VMEM((2, width + 8, 2 * LANES), F32),
+            pltpu.VMEM((2, width + 8, 2 * LANES), F32),
+            pltpu.VMEM((2, width + 8, 2 * LANES), F32),
+            pltpu.VMEM((2, 2, width + 8, LANES), F32),
+            pltpu.VMEM((2, width + 8, 2 * LANES), F32),
+            pltpu.VMEM((2, wide, LANES), F32),
+            pltpu.VMEM((classes, 2, width // 2 + 16, 2 * LANES), BF),
+            pltpu.VMEM((2, 2 * LANES, 2 * LANES), BF),
+            pltpu.VMEM((per_step, 2, readout + 16, 2 * LANES), BF),
+            pltpu.VMEM((per_step, 2 * readout, 2 * LANES), BF),
+            pltpu.SemaphoreType.DMA((len(operands),)),
         ],
-        out_specs=whole(image.shape),
-        out_shape=jax.ShapeDtypeStruct(image.shape, F32),
-        scratch_shapes=[
-            pltpu.VMEM((2, width, 2 * LANES), F32),
-            pltpu.VMEM((2, width, 2 * LANES), F32),
-            pltpu.VMEM((2, width, 2 * LANES), F32),
-            pltpu.VMEM((4, width, LANES), F32),
-            pltpu.VMEM((2, width, 2 * LANES), F32),
-            pltpu.VMEM((2, wide, LANES), F32),
-            pltpu.VMEM((2, classes, width // 2, 2 * LANES), F32),
-            pltpu.VMEM((2, 2 * LANES, 2 * LANES), BF),
-            pltpu.VMEM((per_step, 2, readout, 2 * LANES), BF),
-        ],
-        compiler_params=pltpu.CompilerParams(vmem_limit_bytes=48 * 2**20),
+        compiler_params=pltpu.CompilerParams(vmem_limit_bytes=64 * 2**20 - 2**16),
         name="normal_operator",
-    )(motion, mask, image, psf, coils, jnp.asarray(pads), jnp.asarray(crops), jnp.asarray(tx), jnp.asarray(ty))
+    )(*operands)
 
 
 def from_partner(value, axis, apart):

time: 47.9 us -> 31.2 us (0.65)
  Pallas kernels: 37 us -> 26.9 us
  local copies, waits for them, and re-layouts: 7.53 us -> 0 us
  other arithmetic: 0.82 us -> 1.79 us
    pallas_call x1, Pallas kernels: 37 us -> 26.9 us  [slice_operator(): pl.pallas_call(functools.partial(kernel, length=length, classes=classes,...]
    unnamed x16 -> x0, local copies, waits for them, and re-layouts: 7.53 us -> none
    transpose x1, other arithmetic: 0.82 us -> 1.79 us  [on_device(): return jnp.transpose(total, (2, 0, 1))]
where the time goes in v1:
time: 31.2 us; the launch traced here: 31 us
  Pallas kernels  26.9 us (86%)
  other arithmetic  1.79 us (6%)
  waiting for transfers between devices  1.56 us (5%)
  starting transfers between devices  0.74 us (2%)
    pallas_call x1, Pallas kernels, slice_operator(): pl.pallas_call(functools.partial(kernel, length=length, classes=classes,...  26.9 us
    transpose x1, other arithmetic, on_device(): return jnp.transpose(total, (2, 0, 1))  1.79 us
    ppermute x1, waiting for transfers between devices, on_device(): total = total + lax.ppermute(result, 'shot', pairs)  1.56 us
    ppermute x1, starting transfers between devices, on_device(): total = total + lax.ppermute(result, 'shot', pairs)  0.74 us
  transfers between devices with their start and end apart: 1, of which 1 were waited for; matrix products, arithmetic and copies ran while one was open for 0% of the time, Pallas kernels for 0%

profile of v1, /device:TPU:13, one launch (start us, length us, event | category | flops | bytes accessed | tf_op | source)
XLA Modules:
  0.0 31.0 jit_solution(3688891935670912215)
XLA Ops:
  0.0 26.9 %normal_operator.1 = f32[2,192,200]{2,1,0:T(8,128)} custom-call(s32[1,3]{1,0:T(1,128)} %motion_hbm.1, s32[1,200]{1,0:T(1,128)} %mask_hbm.1, f32[2,192,200]{2,1,0:T(8,128)} %bitcast.5, bf16[2,384,192]{2,1,0:T(8,128)(2,1)} %constant.8.clone.tx_hbm, bf16[2,2,256,256]{3,2,1,0:T(8,128)(2,1)} %constant.9.clone.ty_hbm, f32[200,576]{1,0:T(8,128)} %psf_hbm.1, ...), custom_call_target="tpu_custom_call" | custom-call | tf_op jit(solution)/shard_map/normal_operator/pallas_call | solution.py:325
  26.9 0.7 %collective-permute-start = (f32[2,192,200]{2,1,0:T(8,128)}, f32[2,192,200]{2,1,0:T(8,128)S(1)}, u32[]{:S(2)}, u32[]{:S(2)}) collective-permute-start(f32[2,192,200]{2,1,0:T(8,128)} %normal_operator.1), channel_id=1, source_target_pairs={{0,8},{8,0},{1,9},{9,1},{2,10},{10,2},{3,11},{11,3},{4,12},{12,4},... | collective-permute-start | bytes 921608 | tf_op jit(solution)/shard_map/ppermute | solution.py:422
  27.7 1.6 %collective-permute-done = f32[2,192,200]{2,1,0:T(8,128)S(1)} collective-permute-done((f32[2,192,200]{2,1,0:T(8,128)}, f32[2,192,200]{2,1,0:T(8,128)S(1)}, u32[]{:S(2)}, u32[]{:S(2)}) %collective-permute-start) | collective-permute-done | bytes 307232 | tf_op jit(solution)/shard_map/ppermute | solution.py:422
  29.3 1.8 %add_bitcast_fusion = f32[200,2,192]{0,2,1:T(8,128)} fusion(f32[2,192,200]{2,1,0:T(8,128)} %normal_operator.1, f32[2,192,200]{2,1,0:T(8,128)S(1)} %collective-permute-done), kind=kLoop, calls=%fused_computation | loop fusion | flops 76800 | bytes 921600 | tf_op jit(solution)/shard_map/transpose | solution.py:423
Async XLA Ops:
  26.9 2.3 %collective-permute-start = (f32[2,192,200]{2,1,0:T(8,128)}, f32[2,192,200]{2,1,0:T(8,128)S(1)}, u32[]{:S(2)}, u32[]{:S(2)}) collective-permute-start(f32[2,192,200]{2,1,0:T(8,128)} %normal_operator.1), channel_id=1, source_target_pairs={{0,8},{8,0},{1,9},{9,1},{2,10},{10,2},{3,11},{11,3},{4,12},{12,4},... | collective-permute-start | bytes 921608 | tf_op jit(solution)/shard_map/ppermute | solution.py:422

commit v2 on v1

--- a/solution.py
+++ b/solution.py
@@ -12,6 +12,7 @@
 ANGLE_STEP = 0.02
 SHIFT_STEP = 0.5
 LANES = 128
+UNROLL = 1
 BF = jnp.bfloat16
 F32 = jnp.float32
 
@@ -23,9 +24,14 @@
 
 
 def row_tables(width):
-    index = np.arange(width)
-    angle = 2 * np.pi * (np.outer(index, index) % width) / width
-    return split_pair(np.concatenate([np.cos(angle), np.sin(angle)], 0) / np.sqrt(width))
+    half = width // 2
+    result = []
+    for parity in range(2):
+        freqs = 2 * np.arange(half)[:, None] + parity
+        wave = np.exp(-2j * np.pi * (freqs * np.arange(half)[None, :] % width) / width) / np.sqrt(width)
+        table = np.block([[wave.real, -wave.imag], [wave.imag, wave.real]])
+        result.append([split_pair(table), split_pair(table.T)])
+    return np.array(result, BF)
 
 
 def column_tables(length):
@@ -106,19 +112,25 @@
     return jnp.concatenate([value[:, :half], blank, value[:, half:], blank], 1)
 
 
-def table_rows(tx_ref, value):
+def table_rows(tx_ref, parity, way, value):
     high, low = two(value)
-    return dot(tx_ref[0], high) + dot(tx_ref[1], high) + dot(tx_ref[0], low)
+    th, tl = tx_ref[parity, way, 0], tx_ref[parity, way, 1]
+    return dot(th, high) + dot(tl, high) + dot(th, low)
 
 
 def shear_rows(re, im, tx_ref, phase_ref, sign):
-    width = re.shape[0]
-    from_re, from_im = table_rows(tx_ref, re), table_rows(tx_ref, im)
-    sr = from_re[:width] + from_im[width:]
-    si = from_im[:width] - from_re[width:]
-    c, s = phase_ref[0, :width], phase_ref[1, :width] * sign
-    from_re, from_im = table_rows(tx_ref, sr * c - si * s), table_rows(tx_ref, sr * s + si * c)
-    return from_re[:width] - from_im[width:], from_im[:width] + from_re[width:]
+    half = re.shape[0] // 2
+    back = []
+    for parity in range(2):
+        join = (lambda v: v[:half] - v[half:]) if parity else (lambda v: v[:half] + v[half:])
+        spectra = table_rows(tx_ref, parity, 0, jnp.concatenate([join(re), join(im)], 0))
+        sr, si = spectra[:half], spectra[half:]
+        rows = slice(parity * half, (parity + 1) * half)
+        c, s = phase_ref[0, rows], phase_ref[1, rows] * sign
+        back.append(table_rows(tx_ref, parity, 1, jnp.concatenate([sr * c - si * s, sr * s + si * c], 0)))
+    even, odd = back
+    low, high = even + odd, even - odd
+    return jnp.concatenate([low[:half], high[:half]], 0), jnp.concatenate([low[half:], high[half:]], 0)
 
 
 def shear_columns(re, im, ty_ref, phase_ref, sign):
@@ -161,7 +173,8 @@
     lane = lax.broadcasted_iota(jnp.int32, (1, 2 * LANES), 1)
     line = jnp.where(lane < LANES, lane, lane - LANES + half)
     bend = slope * (line.astype(F32) - length / 2.0)
-    freq = signed(lax.broadcasted_iota(jnp.int32, (width, 1), 0), width) * (-1.0 / width)
+    row = lax.broadcasted_iota(jnp.int32, (width, 1), 0)
+    freq = signed(jnp.where(row < width // 2, 2 * row, 2 * row + 1 - width), width) * (-1.0 / width)
     c, s = turn_pair(wrap(freq * bend))
     put(p3_ref, c, s)
     cx, sx = turn_pair(wrap(freq * shift_x))
@@ -220,11 +233,12 @@
         put(wave_ref.at[j], c.astype(BF), s.astype(BF))
 
 
-def one_coil(coil, rot_ref, acc_ref, pt_ref, ct_ref, wave_ref, h_ref, w_ref, u_ref, length, classes):
+def encode(coil, rot_ref, pt_ref, wave_ref, c_ref, w_ref, length, classes):
     width = coil.shape[1]
     half = width // 2
     cr = spread(coil[0], length)
     ci = spread(coil[1], length)
+    put(c_ref, cr, ci)
     rr, ri = rot_ref[0, :width], rot_ref[1, :width]
     zr = (cr.astype(F32) * rr - ci.astype(F32) * ri).astype(BF)
     zi = (cr.astype(F32) * ri + ci.astype(F32) * rr).astype(BF)
@@ -249,6 +263,9 @@
             w_ref[0, rows, LANES:] = vi[:, :LANES] + vi[:, LANES:]
             w_ref[1, rows, :LANES] = vr[:, :LANES] - vr[:, LANES:]
             w_ref[1, rows, LANES:] = vi[:, :LANES] - vi[:, LANES:]
+
+
+def project(wave_ref, h_ref, w_ref, u_ref, half, classes):
     readout = classes * half
     plus = dot(w_ref[0, :readout], h_ref[0]).astype(BF)
     minus = dot(w_ref[1, :readout], h_ref[1]).astype(BF)
@@ -260,27 +277,34 @@
             c, s = wave_ref[cls, 0, :half, lanes], wave_ref[cls, 1, :half, lanes]
             u_ref[pl.ds(2 * cls * half, half), lanes] = yr * c + yi * s
             u_ref[pl.ds((2 * cls + 1) * half, half), lanes] = yi * c - yr * s
+
+
+def decode(acc_ref, ct_ref, c_ref, u_ref, width):
     back = dot(ct_ref[...], u_ref[...])
     br, bi = back[:width], back[width:]
-    crf, cif = cr.astype(F32), ci.astype(F32)
-    acc_ref[0, :width] += crf * br + cif * bi
-    acc_ref[1, :width] += crf * bi - cif * br
+    cr, ci = c_ref[0, :width].astype(F32), c_ref[1, :width].astype(F32)
+    acc_ref[0, :width] += cr * br + ci * bi
+    acc_ref[1, :width] += cr * bi - ci * br
 
 
 def kernel(
     motion_hbm, mask_hbm, image_hbm, tx_hbm, ty_hbm, psf_hbm, pt_hbm, coil_hbm, ct_hbm, out_ref,
     motion_ref, mask_ref, image_ref, tx_ref, ty_ref, psf_ref, pt_ref, coil_ref, ct_ref,
-    rot_ref, acc_ref, p1_ref, pc_ref, p3_ref, psft_ref, wave_ref, h_ref, w_ref, u_ref, sems,
-    *, length, classes, per_step,
+    rot_ref, acc_ref, p1_ref, pc_ref, p3_ref, psft_ref, wave_ref, h_ref, c_ref, w_ref, u_ref, sems,
+    *, length, classes, unroll,
 ):
     width = image_ref.shape[1]
     half = length // 2
     sources = (motion_hbm, mask_hbm, image_hbm, tx_hbm, ty_hbm, psf_hbm, pt_hbm, coil_hbm, ct_hbm)
     targets = (motion_ref, mask_ref, image_ref, tx_ref, ty_ref, psf_ref, pt_ref, coil_ref, ct_ref)
     copies = [pltpu.make_async_copy(a, b, sems.at[i]) for i, (a, b) in enumerate(zip(sources, targets))]
-    for copy in copies:
+    for copy in copies[:6]:
         copy.start()
-    for copy in copies[:6]:
+    for copy in copies[:4]:
+        copy.wait()
+    for copy in copies[6:]:
+        copy.start()
+    for copy in copies[4:6]:
         copy.wait()
     make_phases(motion_ref, p1_ref, pc_ref, p3_ref, width, length)
     re, im = spread(image_ref[0], length), spread(image_ref[1], length)
@@ -294,15 +318,52 @@
     for copy in copies[6:]:
         copy.wait()
 
-    def some_coils(step, carry):
-        for c in range(per_step):
-            one_coil(
-                coil_ref[step * per_step + c], rot_ref, acc_ref, pt_ref, ct_ref, wave_ref, h_ref,
-                w_ref.at[c], u_ref.at[c], length, classes,
-            )
-        return carry
-
-    lax.fori_loop(0, coil_ref.shape[0] // per_step, some_coils, 0)
+    count = coil_ref.shape[0]
+
+    def run(stage, coil):
+        slot = coil % 2 if isinstance(coil, int) else coil[1]
+        index = coil if isinstance(coil, int) else coil[0]
+        if stage == 0:
+            encode(coil_ref[index], rot_ref, pt_ref, wave_ref, c_ref.at[slot], w_ref.at[slot], length, classes)
+        elif stage == 1:
+            project(wave_ref, h_ref, w_ref.at[slot], u_ref.at[slot], width // 2, classes)
+        else:
+            decode(acc_ref, ct_ref, c_ref.at[slot], u_ref.at[slot], width)
+
+    def pair(first):
+        run(2, (first - 2, 0))
+        run(1, (first - 1, 1))
+        run(0, (first, 0))
+        run(2, (first - 1, 1))
+        run(1, (first, 0))
+        run(0, (first + 1, 1))
+
+    if count % 2:
+        def single(coil, carry):
+            for stage in range(3):
+                run(stage, (coil, 0))
+            return carry
+
+        lax.fori_loop(0, count, single, 0)
+    else:
+        pairs = count // 2 - 1
+        run(0, 0)
+        run(1, 0)
+        run(0, 1)
+        steps = pairs // unroll
+        for extra in range(pairs - steps * unroll):
+            pair(2 * extra + 2)
+
+        def some_pairs(step, carry):
+            for inner in range(unroll):
+                pair(2 * (pairs - steps * unroll + step * unroll + inner) + 2)
+            return carry
+
+        if steps:
+            lax.fori_loop(0, steps, some_pairs, 0)
+        run(2, count - 2)
+        run(1, count - 1)
+        run(2, count - 1)
 
     re, im = acc_ref[0, :width], acc_ref[1, :width]
     re, im = shear_rows(re, im, tx_ref, p3_ref, -1.0)
@@ -315,15 +376,13 @@
 def slice_operator(motion, mask, image, psf, coils):
     _, width, length = image.shape
     readout = psf.shape[1]
-    count = coils.shape[0]
     classes = readout // (width // 2)
     pads, crops = readout_tables(width, readout)
     tx, ty = row_tables(width), column_tables(length)
-    per_step = 2 if count % 2 == 0 else 1
     wide = -(-readout // LANES) * LANES
     operands = (motion, mask, image, jnp.asarray(tx), jnp.asarray(ty), psf, jnp.asarray(pads), coils, jnp.asarray(crops))
     return pl.pallas_call(
-        functools.partial(kernel, length=length, classes=classes, per_step=per_step),
+        functools.partial(kernel, length=length, classes=classes, unroll=UNROLL),
         in_specs=[pl.BlockSpec(memory_space=pltpu.HBM) for _ in operands],
         out_specs=pl.BlockSpec(memory_space=pltpu.VMEM),
         out_shape=jax.ShapeDtypeStruct(image.shape, F32),
@@ -338,13 +397,14 @@
             pltpu.VMEM((2, wide, LANES), F32),
             pltpu.VMEM((classes, 2, width // 2 + 16, 2 * LANES), BF),
             pltpu.VMEM((2, 2 * LANES, 2 * LANES), BF),
-            pltpu.VMEM((per_step, 2, readout + 16, 2 * LANES), BF),
-            pltpu.VMEM((per_step, 2 * readout, 2 * LANES), BF),
+            pltpu.VMEM((2, 2, width + 16, 2 * LANES), BF),
+            pltpu.VMEM((2, 2, readout + 16, 2 * LANES), BF),
+            pltpu.VMEM((2, 2 * readout, 2 * LANES), BF),
             pltpu.SemaphoreType.DMA((len(operands),)),
         ],
-        compiler_params=pltpu.CompilerParams(vmem_limit_bytes=64 * 2**20 - 2**16),
+        compiler_params=pltpu.CompilerParams(vmem_limit_bytes=40 * 2**20),
         name="normal_operator",
-    )(*operands)
+    )(*[pltpu.with_memory_space_constraint(a, pltpu.HBM) for a in operands])
 
 
 def from_partner(value, axis, apart):

time: 31.2 us -> 23.5 us (0.75)
  Pallas kernels: 26.9 us -> 20.4 us
  other arithmetic: 1.79 us -> 0.8 us
    pallas_call x1, Pallas kernels: 26.9 us -> 20.4 us  [slice_operator(): pl.pallas_call(functools.partial(kernel, length=length, classes=classes,...]
    transpose x1, other arithmetic: 1.79 us -> 0.8 us  [on_device(): return jnp.transpose(total, (2, 0, 1))]
where the time goes in v2:
time: 23.5 us; the launch traced here: 23.3 us
  Pallas kernels  20.4 us (87%)
  waiting for transfers between devices  1.35 us (6%)
  other arithmetic  0.8 us (3%)
  starting transfers between devices  0.72 us (3%)
    pallas_call x1, Pallas kernels, slice_operator(): pl.pallas_call(functools.partial(kernel, length=length, classes=classes,...  20.4 us
    ppermute x1, waiting for transfers between devices, on_device(): total = total + lax.ppermute(result, 'shot', pairs)  1.35 us
    transpose x1, other arithmetic, on_device(): return jnp.transpose(total, (2, 0, 1))  0.8 us
    ppermute x1, starting transfers between devices, on_device(): total = total + lax.ppermute(result, 'shot', pairs)  0.72 us
  transfers between devices with their start and end apart: 1, of which 1 were waited for; matrix products, arithmetic and copies ran while one was open for 0% of the time, Pallas kernels for 0%

profile of v2, /device:TPU:13, one launch (start us, length us, event | category | flops | bytes accessed | tf_op | source)
XLA Modules:
  0.0 23.3 jit_solution(15527458665015974056)
XLA Ops:
  0.0 20.4 %normal_operator.1 = f32[2,192,200]{2,1,0:T(8,128)S(1)} custom-call(s32[1,3]{1,0:T(1,128)} %motion_hbm.1, s32[1,200]{1,0:T(1,128)} %mask_hbm.1, f32[2,192,200]{2,1,0:T(8,128)} %bitcast.5, bf16[2,2,2,192,192]{4,3,2,1,0:T(8,128)(2,1)} %constant.8.clone.tx_hbm, bf16[2,2,256,256]{3,2,1,0:T(8,128)(2,1)} %constant.9.clone.ty_hbm, f32[200,576]{1,0:T(8,128)} %psf_hbm.1, ...), custom_call_target="tpu_custom_call" | custom-call | tf_op jit(solution)/shard_map/normal_operator/pallas_call | solution.py:384
  20.4 0.7 %collective-permute-start = (f32[2,192,200]{2,1,0:T(8,128)S(1)}, f32[2,192,200]{2,1,0:T(8,128)S(1)}, u32[]{:S(2)}, u32[]{:S(2)}) collective-permute-start(f32[2,192,200]{2,1,0:T(8,128)S(1)} %normal_operator.1), channel_id=1, source_target_pairs={{0,8},{8,0},{1,9},{9,1},{2,10},{10,2},{3,11},{11,3},{4,12},{12,4},... | collective-permute-start | bytes 921608 | tf_op jit(solution)/shard_map/ppermute | solution.py:482
  21.1 1.3 %collective-permute-done = f32[2,192,200]{2,1,0:T(8,128)S(1)} collective-permute-done((f32[2,192,200]{2,1,0:T(8,128)S(1)}, f32[2,192,200]{2,1,0:T(8,128)S(1)}, u32[]{:S(2)}, u32[]{:S(2)}) %collective-permute-start) | collective-permute-done | bytes 307232 | tf_op jit(solution)/shard_map/ppermute | solution.py:482
  22.5 0.8 %add_bitcast_fusion = f32[200,2,192]{0,2,1:T(8,128)} fusion(f32[2,192,200]{2,1,0:T(8,128)S(1)} %normal_operator.1, f32[2,192,200]{2,1,0:T(8,128)S(1)} %collective-permute-done), kind=kLoop, calls=%fused_computation | loop fusion | flops 76800 | bytes 921600 | tf_op jit(solution)/shard_map/transpose | solution.py:483
Async XLA Ops:
  20.4 2.1 %collective-permute-start = (f32[2,192,200]{2,1,0:T(8,128)S(1)}, f32[2,192,200]{2,1,0:T(8,128)S(1)}, u32[]{:S(2)}, u32[]{:S(2)}) collective-permute-start(f32[2,192,200]{2,1,0:T(8,128)S(1)} %normal_operator.1), channel_id=1, source_target_pairs={{0,8},{8,0},{1,9},{9,1},{2,10},{10,2},{3,11},{11,3},{4,12},{12,4},... | collective-permute-start | bytes 921608 | tf_op jit(solution)/shard_map/ppermute | solution.py:482

commit v3 on v2

--- a/solution.py
+++ b/solution.py
@@ -12,7 +12,7 @@
 ANGLE_STEP = 0.02
 SHIFT_STEP = 0.5
 LANES = 128
-UNROLL = 1
+UNROLL = 7
 BF = jnp.bfloat16
 F32 = jnp.float32
 
@@ -30,8 +30,8 @@
         freqs = 2 * np.arange(half)[:, None] + parity
         wave = np.exp(-2j * np.pi * (freqs * np.arange(half)[None, :] % width) / width) / np.sqrt(width)
         table = np.block([[wave.real, -wave.imag], [wave.imag, wave.real]])
-        result.append([split_pair(table), split_pair(table.T)])
-    return np.array(result, BF)
+        result.append(split_pair(table))
+    return np.stack(result)
 
 
 def column_tables(length):
@@ -54,16 +54,15 @@
 def readout_tables(width, readout):
     half = width // 2
     classes = readout // half
-    pads, crops = [], []
+    pads = []
     for j in range(classes):
         k = np.arange(half)[:, None] * classes + j
-        x = np.arange(width)[None, :]
+        x = np.arange(half)[None, :]
         angle = -2 * np.pi * (k * x % readout) / readout
         cosine = (np.cos(angle) / np.sqrt(readout)).astype(np.float32).astype(BF)
         sine = (np.sin(angle) / np.sqrt(readout)).astype(np.float32).astype(BF)
-        pads.append(np.block([[cosine[:, :half], -sine[:, :half]], [sine[:, :half], cosine[:, :half]]]))
-        crops.append(np.block([[cosine.T, sine.T], [-sine.T, cosine.T]]))
-    return np.stack(pads), np.concatenate(crops, 1)
+        pads.append(np.block([[cosine, -sine], [sine, cosine]]))
+    return np.stack(pads)
 
 
 def turn_polys():
@@ -112,22 +111,22 @@
     return jnp.concatenate([value[:, :half], blank, value[:, half:], blank], 1)
 
 
-def table_rows(tx_ref, parity, way, value):
+def table_rows(table_ref, value):
     high, low = two(value)
-    th, tl = tx_ref[parity, way, 0], tx_ref[parity, way, 1]
+    th, tl = table_ref[0], table_ref[1]
     return dot(th, high) + dot(tl, high) + dot(th, low)
 
 
-def shear_rows(re, im, tx_ref, phase_ref, sign):
+def shear_rows(re, im, tx_ref, txt_ref, phase_ref, sign):
     half = re.shape[0] // 2
     back = []
     for parity in range(2):
         join = (lambda v: v[:half] - v[half:]) if parity else (lambda v: v[:half] + v[half:])
-        spectra = table_rows(tx_ref, parity, 0, jnp.concatenate([join(re), join(im)], 0))
+        spectra = table_rows(tx_ref.at[parity], jnp.concatenate([join(re), join(im)], 0))
         sr, si = spectra[:half], spectra[half:]
         rows = slice(parity * half, (parity + 1) * half)
         c, s = phase_ref[0, rows], phase_ref[1, rows] * sign
-        back.append(table_rows(tx_ref, parity, 1, jnp.concatenate([sr * c - si * s, sr * s + si * c], 0)))
+        back.append(table_rows(txt_ref.at[parity], jnp.concatenate([sr * c - si * s, sr * s + si * c], 0)))
     even, odd = back
     low, high = even + odd, even - odd
     return jnp.concatenate([low[:half], high[:half]], 0), jnp.concatenate([low[half:], high[half:]], 0)
@@ -231,6 +230,25 @@
         picked = pl.ds(j, rows, stride=classes)
         c, s = turn_pair(jnp.concatenate([psft_ref[0, picked, :], psft_ref[1, picked, :]], 1))
         put(wave_ref.at[j], c.astype(BF), s.astype(BF))
+
+
+def make_inverse_rows(tx_ref, txt_ref):
+    for parity in range(2):
+        for part in range(2):
+            txt_ref[parity, part] = tx_ref[parity, part].astype(F32).T.astype(BF)
+
+
+def make_crop(pt_ref, ct_ref, half, classes):
+    for j in range(classes):
+        back = pt_ref[j].astype(F32).T
+        re, im = back[:half], back[half:]
+        angle = 2 * np.pi * j / classes
+        wr, wi = float(np.cos(angle)), float(np.sin(angle))
+        columns = pl.ds(2 * half * j, 2 * half)
+        ct_ref[pl.ds(0, half), columns] = re.astype(BF)
+        ct_ref[pl.ds(half, half), columns] = (re * wr - im * wi).astype(BF)
+        ct_ref[pl.ds(2 * half, half), columns] = im.astype(BF)
+        ct_ref[pl.ds(3 * half, half), columns] = (re * wi + im * wr).astype(BF)
 
 
 def encode(coil, rot_ref, pt_ref, wave_ref, c_ref, w_ref, length, classes):
@@ -288,37 +306,45 @@
 
 
 def kernel(
-    motion_hbm, mask_hbm, image_hbm, tx_hbm, ty_hbm, psf_hbm, pt_hbm, coil_hbm, ct_hbm, out_ref,
-    motion_ref, mask_ref, image_ref, tx_ref, ty_ref, psf_ref, pt_ref, coil_ref, ct_ref,
-    rot_ref, acc_ref, p1_ref, pc_ref, p3_ref, psft_ref, wave_ref, h_ref, c_ref, w_ref, u_ref, sems,
+    motion_hbm, mask_hbm, image_hbm, tx_hbm, ty_hbm, psf_hbm, pt_hbm, coil_hbm, out_ref,
+    motion_ref, mask_ref, image_ref, tx_ref, ty_ref, psf_ref, pt_ref, coil_ref,
+    txt_ref, ct_ref, rot_ref, acc_ref, p1_ref, pc_ref, p3_ref, psft_ref, wave_ref, h_ref, c_ref, w_ref, u_ref, sems,
     *, length, classes, unroll,
 ):
     width = image_ref.shape[1]
     half = length // 2
-    sources = (motion_hbm, mask_hbm, image_hbm, tx_hbm, ty_hbm, psf_hbm, pt_hbm, coil_hbm, ct_hbm)
-    targets = (motion_ref, mask_ref, image_ref, tx_ref, ty_ref, psf_ref, pt_ref, coil_ref, ct_ref)
+    sources = (motion_hbm, mask_hbm, image_hbm, tx_hbm, ty_hbm, psf_hbm, pt_hbm)
+    targets = (motion_ref, mask_ref, image_ref, tx_ref, ty_ref, psf_ref, pt_ref)
     copies = [pltpu.make_async_copy(a, b, sems.at[i]) for i, (a, b) in enumerate(zip(sources, targets))]
-    for copy in copies[:6]:
+    count = coil_ref.shape[0]
+    chunk = 2 - count % 2
+
+    def coil_copy(index):
+        part = pl.ds(index * chunk, chunk)
+        return pltpu.make_async_copy(coil_hbm.at[part], coil_ref.at[part], sems.at[len(sources) + index])
+
+    for copy in copies:
         copy.start()
-    for copy in copies[:4]:
+    copies[0].wait()
+    make_phases(motion_ref, p1_ref, pc_ref, p3_ref, width, length)
+    for copy in copies[1:4]:
         copy.wait()
-    for copy in copies[6:]:
-        copy.start()
-    for copy in copies[4:6]:
+    for index in range(count // chunk):
+        coil_copy(index).start()
+    make_inverse_rows(tx_ref, txt_ref)
+    re, im = spread(image_ref[0], length), spread(image_ref[1], length)
+    re, im = shear_rows(re, im, tx_ref, txt_ref, p1_ref, 1.0)
+    acc_ref[...] = jnp.zeros_like(acc_ref)
+    for copy in copies[4:]:
         copy.wait()
-    make_phases(motion_ref, p1_ref, pc_ref, p3_ref, width, length)
-    re, im = spread(image_ref[0], length), spread(image_ref[1], length)
-    re, im = shear_rows(re, im, tx_ref, p1_ref, 1.0)
-    re, im = shear_columns(re, im, ty_ref, pc_ref, 1.0)
-    re, im = shear_rows(re, im, tx_ref, p3_ref, 1.0)
-    put(rot_ref, re, im)
-    acc_ref[...] = jnp.zeros_like(acc_ref)
+    make_crop(pt_ref, ct_ref, width // 2, classes)
     make_projector(mask_ref, ty_ref, h_ref, length)
     make_wave(psf_ref, psft_ref, wave_ref, length, classes)
-    for copy in copies[6:]:
-        copy.wait()
-
-    count = coil_ref.shape[0]
+    re, im = shear_columns(re, im, ty_ref, pc_ref, 1.0)
+    re, im = shear_rows(re, im, tx_ref, txt_ref, p3_ref, 1.0)
+    put(rot_ref, re, im)
+    for index in range(count // chunk):
+        coil_copy(index).wait()
 
     def run(stage, coil):
         slot = coil % 2 if isinstance(coil, int) else coil[1]
@@ -366,9 +392,9 @@
         run(2, count - 1)
 
     re, im = acc_ref[0, :width], acc_ref[1, :width]
-    re, im = shear_rows(re, im, tx_ref, p3_ref, -1.0)
+    re, im = shear_rows(re, im, tx_ref, txt_ref, p3_ref, -1.0)
     re, im = shear_columns(re, im, ty_ref, pc_ref, -1.0)
-    re, im = shear_rows(re, im, tx_ref, p1_ref, -1.0)
+    re, im = shear_rows(re, im, tx_ref, txt_ref, p1_ref, -1.0)
     for part, value in enumerate((re, im)):
         out_ref[part] = jnp.concatenate([value[:, :half], value[:, LANES:LANES + half]], 1)
 
@@ -377,10 +403,10 @@
     _, width, length = image.shape
     readout = psf.shape[1]
     classes = readout // (width // 2)
-    pads, crops = readout_tables(width, readout)
+    pads = readout_tables(width, readout)
     tx, ty = row_tables(width), column_tables(length)
     wide = -(-readout // LANES) * LANES
-    operands = (motion, mask, image, jnp.asarray(tx), jnp.asarray(ty), psf, jnp.asarray(pads), coils, jnp.asarray(crops))
+    operands = (motion, mask, image, jnp.asarray(tx), jnp.asarray(ty), psf, jnp.asarray(pads), coils)
     return pl.pallas_call(
         functools.partial(kernel, length=length, classes=classes, unroll=UNROLL),
         in_specs=[pl.BlockSpec(memory_space=pltpu.HBM) for _ in operands],
@@ -389,6 +415,8 @@
         scratch_shapes=[pltpu.SMEM(motion.shape, motion.dtype)]
         + [pltpu.VMEM(a.shape, a.dtype) for a in operands[1:]]
         + [
+            pltpu.VMEM(tx.shape, BF),
+            pltpu.VMEM((2 * width, classes * width), BF),
             pltpu.VMEM((2, width + 8, 2 * LANES), F32),
             pltpu.VMEM((2, width + 8, 2 * LANES), F32),
             pltpu.VMEM((2, width + 8, 2 * LANES), F32),
@@ -400,7 +428,7 @@
             pltpu.VMEM((2, 2, width + 16, 2 * LANES), BF),
             pltpu.VMEM((2, 2, readout + 16, 2 * LANES), BF),
             pltpu.VMEM((2, 2 * readout, 2 * LANES), BF),
-            pltpu.SemaphoreType.DMA((len(operands),)),
+            pltpu.SemaphoreType.DMA((len(operands) + coils.shape[0],)),
         ],
         compiler_params=pltpu.CompilerParams(vmem_limit_bytes=40 * 2**20),
         name="normal_operator",

time: 23.5 us -> 21.9 us (0.932)
  Pallas kernels: 20.4 us -> 18.9 us
    pallas_call x1, Pallas kernels: 20.4 us -> 18.9 us  [slice_operator(): pl.pallas_call(functools.partial(kernel, length=length, classes=classes,...]
where the time goes in v3:
time: 21.9 us; the launch traced here: 21.8 us
  Pallas kernels  18.9 us (86%)
  waiting for transfers between devices  1.35 us (6%)
  other arithmetic  0.8 us (4%)
  starting transfers between devices  0.73 us (3%)
    pallas_call x1, Pallas kernels, slice_operator(): pl.pallas_call(functools.partial(kernel, length=length, classes=classes,...  18.9 us
    ppermute x1, waiting for transfers between devices, on_device(): total = total + lax.ppermute(result, 'shot', pairs)  1.35 us
    transpose x1, other arithmetic, on_device(): return jnp.transpose(total, (2, 0, 1))  0.8 us
    ppermute x1, starting transfers between devices, on_device(): total = total + lax.ppermute(result, 'shot', pairs)  0.73 us
  transfers between devices with their start and end apart: 1, of which 1 were waited for; matrix products, arithmetic and copies ran while one was open for 0% of the time, Pallas kernels for 0%

profile of v3, /device:TPU:13, one launch (start us, length us, event | category | flops | bytes accessed | tf_op | source)
XLA Modules:
  0.0 21.8 jit_solution(10890050685174745322)
XLA Ops:
  0.0 18.9 %normal_operator.1 = f32[2,192,200]{2,1,0:T(8,128)S(1)} custom-call(s32[1,3]{1,0:T(1,128)} %motion_hbm.1, s32[1,200]{1,0:T(1,128)} %mask_hbm.1, f32[2,192,200]{2,1,0:T(8,128)} %bitcast.5, bf16[2,2,192,192]{3,2,1,0:T(8,128)(2,1)} %constant.6.clone.tx_hbm, bf16[2,2,256,256]{3,2,1,0:T(8,128)(2,1)} %constant.7.clone.ty_hbm, f32[200,576]{1,0:T(8,128)} %psf_hbm.1, ...), custom_call_target="tpu_custom_call" | custom-call | tf_op jit(solution)/shard_map/normal_operator/pallas_call | solution.py:410
  18.9 0.7 %collective-permute-start = (f32[2,192,200]{2,1,0:T(8,128)S(1)}, f32[2,192,200]{2,1,0:T(8,128)S(1)}, u32[]{:S(2)}, u32[]{:S(2)}) collective-permute-start(f32[2,192,200]{2,1,0:T(8,128)S(1)} %normal_operator.1), channel_id=1, source_target_pairs={{0,8},{8,0},{1,9},{9,1},{2,10},{10,2},{3,11},{11,3},{4,12},{12,4},... | collective-permute-start | bytes 921608 | tf_op jit(solution)/shard_map/ppermute | solution.py:510
  19.6 1.3 %collective-permute-done = f32[2,192,200]{2,1,0:T(8,128)S(1)} collective-permute-done((f32[2,192,200]{2,1,0:T(8,128)S(1)}, f32[2,192,200]{2,1,0:T(8,128)S(1)}, u32[]{:S(2)}, u32[]{:S(2)}) %collective-permute-start) | collective-permute-done | bytes 307232 | tf_op jit(solution)/shard_map/ppermute | solution.py:510
  21.0 0.8 %add_bitcast_fusion = f32[200,2,192]{0,2,1:T(8,128)} fusion(f32[2,192,200]{2,1,0:T(8,128)S(1)} %normal_operator.1, f32[2,192,200]{2,1,0:T(8,128)S(1)} %collective-permute-done), kind=kLoop, calls=%fused_computation | loop fusion | flops 76800 | bytes 921600 | tf_op jit(solution)/shard_map/transpose | solution.py:511
Async XLA Ops:
  18.9 2.1 %collective-permute-start = (f32[2,192,200]{2,1,0:T(8,128)S(1)}, f32[2,192,200]{2,1,0:T(8,128)S(1)}, u32[]{:S(2)}, u32[]{:S(2)}) collective-permute-start(f32[2,192,200]{2,1,0:T(8,128)S(1)} %normal_operator.1), channel_id=1, source_target_pairs={{0,8},{8,0},{1,9},{9,1},{2,10},{10,2},{3,11},{11,3},{4,12},{12,4},... | collective-permute-start | bytes 921608 | tf_op jit(solution)/shard_map/ppermute | solution.py:510

commit v4 on v3

--- a/solution.py
+++ b/solution.py
@@ -65,24 +65,25 @@
     return np.stack(pads)
 
 
-def turn_polys():
+def turn_polys(degree):
     nodes = np.cos(np.pi * (np.arange(400) + 0.5) / 400) * 0.125 + 0.125
     root = np.sqrt(nodes)
     out = []
     for value in (np.cos(2 * np.pi * root), np.sin(2 * np.pi * root) / root):
-        series = np.polynomial.chebyshev.Chebyshev.fit(nodes, value, 6, domain=[0, 0.25])
+        series = np.polynomial.chebyshev.Chebyshev.fit(nodes, value, degree, domain=[0, 0.25])
         out.append([float(c) for c in series.convert(kind=np.polynomial.Polynomial).coef])
     return out
 
 
-COS_POLY, SIN_POLY = turn_polys()
-
-
-def turn_pair(turns):
+FULL_POLY, WAVE_POLY = turn_polys(6), turn_polys(5)
+
+
+def turn_pair(turns, poly=FULL_POLY):
+    cos_poly, sin_poly = poly
     square = turns * turns
-    cosine = jnp.full_like(square, COS_POLY[-1])
-    sine = jnp.full_like(square, SIN_POLY[-1])
-    for c, s in zip(COS_POLY[-2::-1], SIN_POLY[-2::-1]):
+    cosine = jnp.full_like(square, cos_poly[-1])
+    sine = jnp.full_like(square, sin_poly[-1])
+    for c, s in zip(cos_poly[-2::-1], sin_poly[-2::-1]):
         cosine = cosine * square + c
         sine = sine * square + s
     return cosine, sine * turns
@@ -172,19 +173,30 @@
     lane = lax.broadcasted_iota(jnp.int32, (1, 2 * LANES), 1)
     line = jnp.where(lane < LANES, lane, lane - LANES + half)
     bend = slope * (line.astype(F32) - length / 2.0)
-    row = lax.broadcasted_iota(jnp.int32, (width, 1), 0)
-    freq = signed(jnp.where(row < width // 2, 2 * row, 2 * row + 1 - width), width) * (-1.0 / width)
-    c, s = turn_pair(wrap(freq * bend))
-    put(p3_ref, c, s)
-    cx, sx = turn_pair(wrap(freq * shift_x))
-    put(p1_ref, c * cx - s * sx, c * sx + s * cx)
-    along = lax.broadcasted_iota(jnp.int32, (width, 1), 0).astype(F32) - width / 2.0
-    shift = tilt * along + shift_y
+    side = width // 2
+    coarse = signed(16 * lax.broadcasted_iota(jnp.int32, (-(-side // 64) * 8, 1), 0), width) * (-1.0 / width)
+    fine = (2 * lax.broadcasted_iota(jnp.int32, (8, 1), 0)).astype(F32)
+    for ref, shift in ((p1_ref, bend + shift_x), (p3_ref, bend)):
+        gc, gs = turn_pair(wrap(coarse * shift))
+        for parity in range(2):
+            c, s = turn_pair(wrap((fine + parity) * (-1.0 / width) * shift))
+            for a in range(side // 8):
+                rows = pl.ds(parity * side + 8 * a, 8)
+                ac, as_ = gc[a:a + 1], gs[a:a + 1]
+                ref[0, rows] = c * ac - s * as_
+                ref[1, rows] = c * as_ + s * ac
     lane = lax.broadcasted_iota(jnp.int32, (1, LANES), 1)
+    coarse = (8 * lax.broadcasted_iota(jnp.int32, (-(-width // 64) * 8, 1), 0)).astype(F32) - width / 2.0
+    fine = lax.broadcasted_iota(jnp.int32, (8, 1), 0).astype(F32)
     for parity in range(2):
         freq = signed(2 * lane + parity, length) * (-1.0 / length)
-        c, s = turn_pair(wrap(shift * freq))
-        put(pc_ref.at[parity], c, s)
+        gc, gs = turn_pair(wrap((tilt * coarse + shift_y) * freq))
+        c, s = turn_pair(wrap(tilt * fine * freq))
+        for a in range(width // 8):
+            rows = pl.ds(8 * a, 8)
+            ac, as_ = gc[a:a + 1], gs[a:a + 1]
+            pc_ref[parity, 0, rows] = c * ac - s * as_
+            pc_ref[parity, 1, rows] = c * as_ + s * ac
 
 
 def make_projector(mask_ref, ty_ref, h_ref, length):
@@ -228,7 +240,7 @@
     rows = readout // classes
     for j in range(classes):
         picked = pl.ds(j, rows, stride=classes)
-        c, s = turn_pair(jnp.concatenate([psft_ref[0, picked, :], psft_ref[1, picked, :]], 1))
+        c, s = turn_pair(jnp.concatenate([psft_ref[0, picked, :], psft_ref[1, picked, :]], 1), WAVE_POLY)
         put(wave_ref.at[j], c.astype(BF), s.astype(BF))
 
 
@@ -299,10 +311,10 @@
 
 def decode(acc_ref, ct_ref, c_ref, u_ref, width):
     back = dot(ct_ref[...], u_ref[...])
-    br, bi = back[:width], back[width:]
-    cr, ci = c_ref[0, :width].astype(F32), c_ref[1, :width].astype(F32)
-    acc_ref[0, :width] += cr * br + ci * bi
-    acc_ref[1, :width] += cr * bi - ci * br
+    br, bi = back[:width].astype(BF), back[width:].astype(BF)
+    cr, ci = c_ref[0, :width], c_ref[1, :width]
+    acc_ref[0, :width] += (cr * br + ci * bi).astype(F32)
+    acc_ref[1, :width] += (cr * bi - ci * br).astype(F32)
 
 
 def kernel(
@@ -339,9 +351,9 @@
         copy.wait()
     make_crop(pt_ref, ct_ref, width // 2, classes)
     make_projector(mask_ref, ty_ref, h_ref, length)
-    make_wave(psf_ref, psft_ref, wave_ref, length, classes)
     re, im = shear_columns(re, im, ty_ref, pc_ref, 1.0)
     re, im = shear_rows(re, im, tx_ref, txt_ref, p3_ref, 1.0)
+    make_wave(psf_ref, psft_ref, wave_ref, length, classes)
     put(rot_ref, re, im)
     for index in range(count // chunk):
         coil_copy(index).wait()

time: 21.9 us -> 21.1 us (0.963)
  Pallas kernels: 18.9 us -> 18 us
    pallas_call x1, Pallas kernels: 18.9 us -> 18 us  [slice_operator(): pl.pallas_call(functools.partial(kernel, length=length, classes=classes,...]
where the time goes in v4:
time: 21.1 us; the launch traced here: 20.9 us
  Pallas kernels  18 us (85%)
  waiting for transfers between devices  1.35 us (6%)
  other arithmetic  0.8 us (4%)
  starting transfers between devices  0.75 us (4%)
    pallas_call x1, Pallas kernels, slice_operator(): pl.pallas_call(functools.partial(kernel, length=length, classes=classes,...  18 us
    ppermute x1, waiting for transfers between devices, on_device(): total = total + lax.ppermute(result, 'shot', pairs)  1.35 us
    transpose x1, other arithmetic, on_device(): return jnp.transpose(total, (2, 0, 1))  0.8 us
    ppermute x1, starting transfers between devices, on_device(): total = total + lax.ppermute(result, 'shot', pairs)  0.75 us
  transfers between devices with their start and end apart: 1, of which 1 were waited for; matrix products, arithmetic and copies ran while one was open for 0% of the time, Pallas kernels for 0%

profile of v4, /device:TPU:13, one launch (start us, length us, event | category | flops | bytes accessed | tf_op | source)
XLA Modules:
  0.0 20.9 jit_solution(13320269002075280706)
XLA Ops:
  0.0 18.0 %normal_operator.1 = f32[2,192,200]{2,1,0:T(8,128)S(1)} custom-call(s32[1,3]{1,0:T(1,128)} %motion_hbm.1, s32[1,200]{1,0:T(1,128)} %mask_hbm.1, f32[2,192,200]{2,1,0:T(8,128)} %bitcast.5, bf16[2,2,192,192]{3,2,1,0:T(8,128)(2,1)} %constant.6.clone.tx_hbm, bf16[2,2,256,256]{3,2,1,0:T(8,128)(2,1)} %constant.7.clone.ty_hbm, f32[200,576]{1,0:T(8,128)} %psf_hbm.1, ...), custom_call_target="tpu_custom_call" | custom-call | tf_op jit(solution)/shard_map/normal_operator/pallas_call | solution.py:422
  18.0 0.7 %collective-permute-start = (f32[2,192,200]{2,1,0:T(8,128)S(1)}, f32[2,192,200]{2,1,0:T(8,128)S(1)}, u32[]{:S(2)}, u32[]{:S(2)}) collective-permute-start(f32[2,192,200]{2,1,0:T(8,128)S(1)} %normal_operator.1), channel_id=1, source_target_pairs={{0,8},{8,0},{1,9},{9,1},{2,10},{10,2},{3,11},{11,3},{4,12},{12,4},... | collective-permute-start | bytes 921608 | tf_op jit(solution)/shard_map/ppermute | solution.py:522
  18.8 1.3 %collective-permute-done = f32[2,192,200]{2,1,0:T(8,128)S(1)} collective-permute-done((f32[2,192,200]{2,1,0:T(8,128)S(1)}, f32[2,192,200]{2,1,0:T(8,128)S(1)}, u32[]{:S(2)}, u32[]{:S(2)}) %collective-permute-start) | collective-permute-done | bytes 307232 | tf_op jit(solution)/shard_map/ppermute | solution.py:522
  20.1 0.8 %add_bitcast_fusion = f32[200,2,192]{0,2,1:T(8,128)} fusion(f32[2,192,200]{2,1,0:T(8,128)S(1)} %normal_operator.1, f32[2,192,200]{2,1,0:T(8,128)S(1)} %collective-permute-done), kind=kLoop, calls=%fused_computation | loop fusion | flops 76800 | bytes 921600 | tf_op jit(solution)/shard_map/transpose | solution.py:523
Async XLA Ops:
  18.0 2.1 %collective-permute-start = (f32[2,192,200]{2,1,0:T(8,128)S(1)}, f32[2,192,200]{2,1,0:T(8,128)S(1)}, u32[]{:S(2)}, u32[]{:S(2)}) collective-permute-start(f32[2,192,200]{2,1,0:T(8,128)S(1)} %normal_operator.1), channel_id=1, source_target_pairs={{0,8},{8,0},{1,9},{9,1},{2,10},{10,2},{3,11},{11,3},{4,12},{12,4},... | collective-permute-start | bytes 921608 | tf_op jit(solution)/shard_map/ppermute | solution.py:522

commit v5 on v4

--- a/solution.py
+++ b/solution.py
@@ -297,10 +297,14 @@
 
 def project(wave_ref, h_ref, w_ref, u_ref, half, classes):
     readout = classes * half
-    plus = dot(w_ref[0, :readout], h_ref[0]).astype(BF)
-    minus = dot(w_ref[1, :readout], h_ref[1]).astype(BF)
+    third = readout // 3
+    pieces = [
+        (dot(w_ref[0, i:i + third], h_ref[0]).astype(BF), dot(w_ref[1, i:i + third], h_ref[1]).astype(BF))
+        for i in range(0, readout, third)
+    ]
     for cls in range(classes):
-        rows = slice(cls * half, (cls + 1) * half)
+        plus, minus = pieces[cls * half // third]
+        rows = slice(cls * half % third, cls * half % third + half)
         for side, y in enumerate((plus[rows] + minus[rows], plus[rows] - minus[rows])):
             lanes = slice(side * LANES, (side + 1) * LANES)
             yr, yi = y[:, :LANES], y[:, LANES:]

time: 21.1 us -> 20.7 us (0.981)
  Pallas kernels: 18 us -> 17.6 us
    pallas_call x1, Pallas kernels: 18 us -> 17.6 us  [slice_operator(): pl.pallas_call(functools.partial(kernel, length=length, classes=classes,...]
where the time goes in v5:
time: 20.7 us; the launch traced here: 20.5 us
  Pallas kernels  17.6 us (85%)
  waiting for transfers between devices  1.35 us (7%)
  other arithmetic  0.8 us (4%)
  starting transfers between devices  0.75 us (4%)
    pallas_call x1, Pallas kernels, slice_operator(): pl.pallas_call(functools.partial(kernel, length=length, classes=classes,...  17.6 us
    ppermute x1, waiting for transfers between devices, on_device(): total = total + lax.ppermute(result, 'shot', pairs)  1.35 us
    transpose x1, other arithmetic, on_device(): return jnp.transpose(total, (2, 0, 1))  0.8 us
    ppermute x1, starting transfers between devices, on_device(): total = total + lax.ppermute(result, 'shot', pairs)  0.75 us
  transfers between devices with their start and end apart: 1, of which 1 were waited for; matrix products, arithmetic and copies ran while one was open for 0% of the time, Pallas kernels for 0%

profile of v5, /device:TPU:13, one launch (start us, length us, event | category | flops | bytes accessed | tf_op | source)
XLA Modules:
  0.0 20.5 jit_solution(5128011079910927060)
XLA Ops:
  0.0 17.6 %normal_operator.1 = f32[2,192,200]{2,1,0:T(8,128)S(1)} custom-call(s32[1,3]{1,0:T(1,128)} %motion_hbm.1, s32[1,200]{1,0:T(1,128)} %mask_hbm.1, f32[2,192,200]{2,1,0:T(8,128)} %bitcast.5, bf16[2,2,192,192]{3,2,1,0:T(8,128)(2,1)} %constant.6.clone.tx_hbm, bf16[2,2,256,256]{3,2,1,0:T(8,128)(2,1)} %constant.7.clone.ty_hbm, f32[200,576]{1,0:T(8,128)} %psf_hbm.1, ...), custom_call_target="tpu_custom_call" | custom-call | tf_op jit(solution)/shard_map/normal_operator/pallas_call | solution.py:426
  17.6 0.7 %collective-permute-start = (f32[2,192,200]{2,1,0:T(8,128)S(1)}, f32[2,192,200]{2,1,0:T(8,128)S(1)}, u32[]{:S(2)}, u32[]{:S(2)}) collective-permute-start(f32[2,192,200]{2,1,0:T(8,128)S(1)} %normal_operator.1), channel_id=1, source_target_pairs={{0,8},{8,0},{1,9},{9,1},{2,10},{10,2},{3,11},{11,3},{4,12},{12,4},... | collective-permute-start | bytes 921608 | tf_op jit(solution)/shard_map/ppermute | solution.py:526
  18.4 1.3 %collective-permute-done = f32[2,192,200]{2,1,0:T(8,128)S(1)} collective-permute-done((f32[2,192,200]{2,1,0:T(8,128)S(1)}, f32[2,192,200]{2,1,0:T(8,128)S(1)}, u32[]{:S(2)}, u32[]{:S(2)}) %collective-permute-start) | collective-permute-done | bytes 307232 | tf_op jit(solution)/shard_map/ppermute | solution.py:526
  19.7 0.8 %add_bitcast_fusion = f32[200,2,192]{0,2,1:T(8,128)} fusion(f32[2,192,200]{2,1,0:T(8,128)S(1)} %normal_operator.1, f32[2,192,200]{2,1,0:T(8,128)S(1)} %collective-permute-done), kind=kLoop, calls=%fused_computation | loop fusion | flops 76800 | bytes 921600 | tf_op jit(solution)/shard_map/transpose | solution.py:527
Async XLA Ops:
  17.6 2.1 %collective-permute-start = (f32[2,192,200]{2,1,0:T(8,128)S(1)}, f32[2,192,200]{2,1,0:T(8,128)S(1)}, u32[]{:S(2)}, u32[]{:S(2)}) collective-permute-start(f32[2,192,200]{2,1,0:T(8,128)S(1)} %normal_operator.1), channel_id=1, source_target_pairs={{0,8},{8,0},{1,9},{9,1},{2,10},{10,2},{3,11},{11,3},{4,12},{12,4},... | collective-permute-start | bytes 921608 | tf_op jit(solution)/shard_map/ppermute | solution.py:526

commit v6 on v5

--- a/solution.py
+++ b/solution.py
@@ -297,7 +297,7 @@
 
 def project(wave_ref, h_ref, w_ref, u_ref, half, classes):
     readout = classes * half
-    third = readout // 3
+    third = readout // classes
     pieces = [
         (dot(w_ref[0, i:i + third], h_ref[0]).astype(BF), dot(w_ref[1, i:i + third], h_ref[1]).astype(BF))
         for i in range(0, readout, third)

time: 20.7 us -> 22.2 us (1.072)
  Pallas kernels: 17.6 us -> 19.1 us
    pallas_call x1, Pallas kernels: 17.6 us -> 19.1 us  [slice_operator(): pl.pallas_call(functools.partial(kernel, length=length, classes=classes,...]
where the time goes in v6:
time: 22.2 us; the launch traced here: 22 us
  Pallas kernels  19.1 us (86%)
  waiting for transfers between devices  1.35 us (6%)
  other arithmetic  0.8 us (4%)
  starting transfers between devices  0.75 us (3%)
    pallas_call x1, Pallas kernels, slice_operator(): pl.pallas_call(functools.partial(kernel, length=length, classes=classes,...  19.1 us
    ppermute x1, waiting for transfers between devices, on_device(): total = total + lax.ppermute(result, 'shot', pairs)  1.35 us
    transpose x1, other arithmetic, on_device(): return jnp.transpose(total, (2, 0, 1))  0.8 us
    ppermute x1, starting transfers between devices, on_device(): total = total + lax.ppermute(result, 'shot', pairs)  0.75 us
  transfers between devices with their start and end apart: 1, of which 1 were waited for; matrix products, arithmetic and copies ran while one was open for 0% of the time, Pallas kernels for 0%

profile of v6, /device:TPU:13, one launch (start us, length us, event | category | flops | bytes accessed | tf_op | source)
XLA Modules:
  0.0 22.0 jit_solution(11416775796892910291)
XLA Ops:
  0.0 19.1 %normal_operator.1 = f32[2,192,200]{2,1,0:T(8,128)S(1)} custom-call(s32[1,3]{1,0:T(1,128)} %motion_hbm.1, s32[1,200]{1,0:T(1,128)} %mask_hbm.1, f32[2,192,200]{2,1,0:T(8,128)} %bitcast.5, bf16[2,2,192,192]{3,2,1,0:T(8,128)(2,1)} %constant.6.clone.tx_hbm, bf16[2,2,256,256]{3,2,1,0:T(8,128)(2,1)} %constant.7.clone.ty_hbm, f32[200,576]{1,0:T(8,128)} %psf_hbm.1, ...), custom_call_target="tpu_custom_call" | custom-call | tf_op jit(solution)/shard_map/normal_operator/pallas_call | solution.py:426
  19.1 0.7 %collective-permute-start = (f32[2,192,200]{2,1,0:T(8,128)S(1)}, f32[2,192,200]{2,1,0:T(8,128)S(1)}, u32[]{:S(2)}, u32[]{:S(2)}) collective-permute-start(f32[2,192,200]{2,1,0:T(8,128)S(1)} %normal_operator.1), channel_id=1, source_target_pairs={{0,8},{8,0},{1,9},{9,1},{2,10},{10,2},{3,11},{11,3},{4,12},{12,4},... | collective-permute-start | bytes 921608 | tf_op jit(solution)/shard_map/ppermute | solution.py:526
  19.9 1.3 %collective-permute-done = f32[2,192,200]{2,1,0:T(8,128)S(1)} collective-permute-done((f32[2,192,200]{2,1,0:T(8,128)S(1)}, f32[2,192,200]{2,1,0:T(8,128)S(1)}, u32[]{:S(2)}, u32[]{:S(2)}) %collective-permute-start) | collective-permute-done | bytes 307232 | tf_op jit(solution)/shard_map/ppermute | solution.py:526
  21.2 0.8 %add_bitcast_fusion = f32[200,2,192]{0,2,1:T(8,128)} fusion(f32[2,192,200]{2,1,0:T(8,128)S(1)} %normal_operator.1, f32[2,192,200]{2,1,0:T(8,128)S(1)} %collective-permute-done), kind=kLoop, calls=%fused_computation | loop fusion | flops 76800 | bytes 921600 | tf_op jit(solution)/shard_map/transpose | solution.py:527
Async XLA Ops:
  19.1 2.1 %collective-permute-start = (f32[2,192,200]{2,1,0:T(8,128)S(1)}, f32[2,192,200]{2,1,0:T(8,128)S(1)}, u32[]{:S(2)}, u32[]{:S(2)}) collective-permute-start(f32[2,192,200]{2,1,0:T(8,128)S(1)} %normal_operator.1), channel_id=1, source_target_pairs={{0,8},{8,0},{1,9},{9,1},{2,10},{10,2},{3,11},{11,3},{4,12},{12,4},... | collective-permute-start | bytes 921608 | tf_op jit(solution)/shard_map/ppermute | solution.py:526
